TPU v7x, 8 devices: a whole 2x2x1 slice. The times are simulated.
8 devices in a mesh: dp: 1 (over z), pz: 2 (over y), py: 4 (over x, core).
Axes of the slice: x: 2, y: 2, z: 1, core: 2. Of those that a mesh axis runs over, the one named last changes fastest.
Arguments:
- rho_re: float32 [32, 64, 64, 64], P('dp', None, 'py', 'pz')
- rho_im: float32 [32, 64, 64, 64], P('dp', None, 'py', 'pz')
- g_re: float32 [64, 64, 64], P('py', 'pz')
- g_im: float32 [64, 64, 64], P('py', 'pz')
Outputs:
- output 1: float32 [32, 64, 64, 64], P('dp', None, 'py', 'pz')
- output 2: float32 [32, 64, 64, 64], P('dp', None, 'py', 'pz')
- output 3: float32 [32, 64, 64, 64], P('dp', 'py', 'pz')
- output 4: float32 [32, 64, 64, 64], P('dp', 'py', 'pz')
All inputs are finite; a program needn't handle non-finite values.
Results may differ from a plain program's by a relative error of at most 0.001.
Values sent between devices are 32-bit elements.
A program may use at most 1 GiB of HBM per device.

v0:
```python
import jax
import jax.numpy as jnp
from jax import lax
from jax.sharding import PartitionSpec as P


def regroup(volume, axis_name, split_dim, concat_dim):
    halves = jnp.stack([jnp.real(volume), jnp.imag(volume)])
    arrived = lax.all_to_all(halves, axis_name, split_dim + 1, concat_dim + 1, tiled=True)
    return lax.complex(arrived[0], arrived[1])


def solution(mesh):
    def local_solve(rho_re, rho_im, g_re, g_im):
        volume = jnp.fft.fft(lax.complex(rho_re, rho_im), axis=1, norm="ortho")
        volume = regroup(volume, "py", 1, 2)
        volume = jnp.fft.fft(volume, axis=2, norm="ortho")
        volume = regroup(volume, "pz", 2, 3)
        spectrum = jnp.fft.fft(volume, axis=3, norm="ortho") * lax.complex(g_re, g_im)
        volume = jnp.fft.ifft(spectrum, axis=3, norm="ortho")
        volume = regroup(volume, "pz", 3, 2)
        volume = jnp.fft.ifft(volume, axis=2, norm="ortho")
        volume = regroup(volume, "py", 2, 1)
        volume = jnp.fft.ifft(volume, axis=1, norm="ortho")
        return jnp.real(volume), jnp.imag(volume), jnp.real(spectrum), jnp.imag(spectrum)

    space_layout = P("dp", None, "py", "pz")
    wave_layout = P("dp", "py", "pz", None)
    green_layout = P("py", "pz", None)
    return jax.shard_map(local_solve, mesh=mesh,
                         in_specs=(space_layout, space_layout, green_layout, green_layout),
                         out_specs=(space_layout, space_layout, wave_layout, wave_layout),
                         check_vma=False)
```

profile of v0, /device:TPU:0, one launch (start us, length us, event | category | flops | bytes accessed | tf_op | source)
XLA Modules:
  0.0 1592.0 jit_solution(9870607263378281401)
XLA Ops:
  50.5 30.4 %copy.42 = f32[2,32,64,16,32]{4,3,1,0,2:T(8,128)} copy(f32[2,32,64,16,32]{2,4,3,1,0:T(8,128)} %pad_maximum_fusion) | data formatting | bytes 16777216 | tf_op jit(solution)/shard_map/stack | solution.py:8
  80.9 33.6 %reshape.98 = f32[4,1,524288]{2,1,0:T(1,128)} reshape(f32[64,2,32,16,32]{4,3,2,1,0:T(8,128)} %bitcast.303) | data formatting | bytes 16777216
  114.5 101.3 %all_to_all.56 = f32[4,1,524288]{2,1,0:T(1,128)} all-to-all(f32[4,1,524288]{2,1,0:T(1,128)} %reshape.98), channel_id=1, replica_groups=mesh['dp'=1,'pz'=2,'py'=4] {'py'}, dimensions={0} | all-to-all | bytes 16777216 | tf_op jit(solution)/shard_map/all_to_all | solution.py:9
  216.4 28.7 %reduce.6 = f32[4,524288]{1,0:T(4,128)} reduce(f32[4,1,524288]{2,1,0:T(1,128)} %all_to_all.56, f32[]{:T(128)} %broadcast.228), dimensions={1}, to_apply=%all_to_all.40.reduce_sub_computation | reduce | bytes 16777220 | tf_op jit(solution)/shard_map/all_to_all | solution.py:9
  245.1 42.4 %reshape.99 = f32[64,2,32,16,32]{4,3,2,1,0:T(8,128)} reshape(f32[4,524288]{1,0:T(4,128)} %reduce.6) | data formatting | bytes 16777216
  287.5 22.8 %copy.43 = f32[2,32,64,16,32]{4,3,2,1,0:T(8,128)} copy(f32[2,32,64,16,32]{4,3,1,0,2:T(8,128)} %bitcast.307) | data formatting | bytes 16777216 | tf_op jit(solution)/shard_map/all_to_all | solution.py:9
  310.3 17.8 %fusion.157 = (f32[1,32,16,4,16,32]{5,4,2,3,1,0:T(8,128)S(1)}, f32[1,32,16,4,16,32]{5,4,2,3,1,0:T(8,128)}) fusion(f32[2,32,16,4,16,32]{5,4,2,3,1,0:T(8,128)} %bitcast.311), kind=kLoop, calls=%fused_computation.180 | loop fusion | bytes 16777216 | tf_op jit(solution)/shard_map/slice | solution.py:10
  420.3 30.4 %copy.48 = f32[2,32,16,64,32]{4,2,1,0,3:T(8,128)} copy(f32[2,32,16,64,32]{3,4,2,1,0:T(8,128)} %pad_maximum_fusion.1) | data formatting | bytes 16777216 | tf_op jit(solution)/shard_map/stack | solution.py:8
  450.8 30.6 %reshape.100 = f32[2,1,1048576]{2,1,0:T(1,128)} reshape(f32[64,2,32,16,32]{4,3,2,1,0:T(8,128)} %bitcast.304) | data formatting | bytes 16777216
  488.3 92.6 %all-to-all-done.1 = f32[2,1,1048576]{2,1,0:T(1,128)} async-done(((f32[2,1,1048576]{2,1,0:T(1,128)}), f32[2,1,1048576]{2,1,0:T(1,128)}, u32[]{:S(2)}, u32[]{:S(2)}) %all-to-all-start.1) | async-done | bytes 8388640 | tf_op jit(solution)/shard_map/all_to_all | solution.py:9
  580.9 31.1 %reduce.7 = f32[2,1048576]{1,0:T(2,128)} reduce(f32[2,1,1048576]{2,1,0:T(1,128)} %all-to-all-done.1, f32[]{:T(128)} %broadcast.228), dimensions={1}, to_apply=%all_to_all.43.reduce_sub_computation | reduce | bytes 16777220 | tf_op jit(solution)/shard_map/all_to_all | solution.py:9
  611.9 33.7 %reshape.101 = f32[64,2,32,16,32]{4,3,2,1,0:T(8,128)} reshape(f32[2,1048576]{1,0:T(2,128)} %reduce.7) | data formatting | bytes 16777216
  645.6 55.1 %copy.73 = f32[2,32,16,2,32,32]{5,3,4,2,1,0:T(2,128)} copy(f32[2,32,16,2,32,32]{5,2,1,0,4,3:T(8,128)} %bitcast.308) | data formatting | bytes 16777216 | tf_op jit(solution)/shard_map/all_to_all | solution.py:9
  700.7 22.8 %fusion.156 = (f32[1,32,16,32,2,32]{5,4,3,2,1,0:T(2,128)}, f32[1,32,16,32,2,32]{5,4,3,2,1,0:T(2,128)}) fusion(f32[2,32,16,32,2,32]{5,4,3,2,1,0:T(2,128)} %bitcast.312), kind=kLoop, calls=%fused_computation.179 | loop fusion | bytes 16777216 | tf_op jit(solution)/shard_map/slice | solution.py:10
  723.5 16.4 %squeeze.27 = f32[32,16,32,64]{3,2,1,0:T(8,128)} reshape(f32[1,32,16,32,2,32]{5,4,3,2,1,0:T(2,128)} %get-tuple-element.112) | data formatting | bytes 8388608 | tf_op jit(solution)/shard_map/squeeze | solution.py:10
  739.9 16.3 %squeeze.26 = f32[32,16,32,64]{3,2,1,0:T(8,128)} reshape(f32[1,32,16,32,2,32]{5,4,3,2,1,0:T(2,128)} %get-tuple-element.113) | data formatting | bytes 8388608 | tf_op jit(solution)/shard_map/squeeze | solution.py:10
  777.1 19.7 %multiply_add_fusion.6 = (f32[32,16,32,64]{3,2,1,0:T(8,128)}, f32[32,16,32,64]{3,2,1,0:T(8,128)}) fusion(f32[16,32,64]{2,1,0:T(8,128)S(1)} %copy-done.10, f32[16,32,64]{2,1,0:T(8,128)S(1)} %copy-done.11, f32[32,16,32,64]{3,2,1,0:T(8,128)} %fusion.48, f32[32,16,32,64]{3,2,1,0:T(8,128)} %fusion.52, f32[32,16,32,64]{3,2,1,0:T(8,128)} %squeeze.26, ...), kind=kOutput, calls=%fused_computation.62 | convolution fusion | flops 821051392 | bytes 25427968 | tf_op jit(solution)/shard_map/jit(fft) | solution.py:19
  847.0 30.4 %copy.50 = f32[2,32,16,32,64]{3,2,1,0,4:T(8,128)} copy(f32[2,32,16,32,64]{4,3,2,1,0:T(8,128)} %pad_maximum_fusion.2) | data formatting | bytes 16777216 | tf_op jit(solution)/shard_map/stack | solution.py:8
  877.4 30.4 %reshape.102 = f32[2,1,1048576]{2,1,0:T(1,128)} reshape(f32[64,2,32,16,32]{4,3,2,1,0:T(8,128)} %bitcast.305) | data formatting | bytes 16777216
  907.8 102.5 %all_to_all.57 = f32[2,1,1048576]{2,1,0:T(1,128)} all-to-all(f32[2,1,1048576]{2,1,0:T(1,128)} %reshape.102), channel_id=1, replica_groups=mesh['dp'=1,'pz'=2,'py'=4] {'pz'}, dimensions={0} | all-to-all | bytes 16777216 | tf_op jit(solution)/shard_map/all_to_all | solution.py:9
  1010.3 31.3 %reduce.8 = f32[2,1048576]{1,0:T(2,128)} reduce(f32[2,1,1048576]{2,1,0:T(1,128)} %all_to_all.57, f32[]{:T(128)} %broadcast.228), dimensions={1}, to_apply=%all_to_all.46.reduce_sub_computation | reduce | bytes 16777220 | tf_op jit(solution)/shard_map/all_to_all | solution.py:9
  1041.6 33.6 %reshape.103 = f32[64,2,32,16,32]{4,3,2,1,0:T(8,128)} reshape(f32[2,1048576]{1,0:T(2,128)} %reduce.8) | data formatting | bytes 16777216
  1075.2 55.1 %copy.72 = f32[2,32,16,32,2,32]{3,4,5,2,1,0:T(2,128)} copy(f32[2,32,16,32,2,32]{3,2,1,0,5,4:T(8,128)} %bitcast.309) | data formatting | bytes 16777216 | tf_op jit(solution)/shard_map/all_to_all | solution.py:9
  1130.3 22.8 %fusion.155 = (f32[1,32,16,2,32,32]{4,3,5,2,1,0:T(2,128)}, f32[1,32,16,2,32,32]{4,3,5,2,1,0:T(2,128)}) fusion(f32[2,32,16,2,32,32]{4,3,5,2,1,0:T(2,128)} %bitcast.313), kind=kLoop, calls=%fused_computation.178 | loop fusion | bytes 16777216 | tf_op jit(solution)/shard_map/slice | solution.py:10
  1153.1 16.4 %squeeze.28 = f32[32,16,64,32]{2,3,1,0:T(8,128)} reshape(f32[1,32,16,2,32,32]{4,3,5,2,1,0:T(2,128)} %get-tuple-element.110) | data formatting | bytes 8388608 | tf_op jit(solution)/shard_map/squeeze | solution.py:10
  1236.4 30.4 %copy.52 = f32[2,32,16,64,32]{4,2,1,0,3:T(8,128)} copy(f32[2,32,16,64,32]{3,4,2,1,0:T(8,128)} %pad_maximum_fusion.3) | data formatting | bytes 16777216 | tf_op jit(solution)/shard_map/stack | solution.py:8
  1266.8 33.4 %reshape.104 = f32[4,1,524288]{2,1,0:T(1,128)} reshape(f32[64,2,32,16,32]{4,3,2,1,0:T(8,128)} %bitcast.306) | data formatting | bytes 16777216
  1300.2 100.3 %all_to_all.58 = f32[4,1,524288]{2,1,0:T(1,128)} all-to-all(f32[4,1,524288]{2,1,0:T(1,128)} %reshape.104), channel_id=1, replica_groups=mesh['dp'=1,'pz'=2,'py'=4] {'py'}, dimensions={0} | all-to-all | bytes 16777216 | tf_op jit(solution)/shard_map/all_to_all | solution.py:9
  1400.5 28.5 %reduce.9 = f32[4,524288]{1,0:T(4,128)} reduce(f32[4,1,524288]{2,1,0:T(1,128)} %all_to_all.58, f32[]{:T(128)} %broadcast.228), dimensions={1}, to_apply=%all_to_all.49.reduce_sub_computation | reduce | bytes 16777220 | tf_op jit(solution)/shard_map/all_to_all | solution.py:9
  1429.0 30.9 %reshape.105 = f32[64,2,32,16,32]{4,3,2,1,0:T(8,128)} reshape(f32[4,524288]{1,0:T(4,128)} %reduce.9) | data formatting | bytes 16777216
  1459.9 31.8 %copy.53 = f32[2,32,16,64,32]{4,3,2,1,0:T(8,128)} copy(f32[2,32,16,64,32]{4,2,1,0,3:T(8,128)} %bitcast.310) | data formatting | bytes 16777216 | tf_op jit(solution)/shard_map/all_to_all | solution.py:9
  1491.7 16.9 %fusion.154 = (f32[1,32,4,16,16,32]{5,4,2,3,1,0:T(8,128)S(1)}, f32[1,32,4,16,16,32]{5,4,2,3,1,0:T(8,128)}) fusion(f32[2,32,4,16,16,32]{5,4,2,3,1,0:T(8,128)} %bitcast.314), kind=kLoop, calls=%fused_computation.177 | loop fusion | bytes 16777216 | tf_op jit(solution)/shard_map/slice | solution.py:10
  (56 shorter events, 370.4 us)
Async XLA Ops:
  0.6 12.5 copy-start.9
  0.6 12.5 copy-start.8
  371.6 9.7 copy-start.1
  481.3 99.5 %all-to-all-start.1 = ((f32[2,1,1048576]{2,1,0:T(1,128)}), f32[2,1,1048576]{2,1,0:T(1,128)}, u32[]{:S(2)}, u32[]{:S(2)}) async-start(f32[2,1,1048576]{2,1,0:T(1,128)} %reshape.100), calls=%async_computation.1 | async-start | bytes 16777216 | tf_op jit(solution)/shard_map/all_to_all | solution.py:9
  756.3 11.7 copy-start
  768.0 9.2 copy-start.10
  768.0 9.2 copy-start.11
  796.9 12.7 copy-start.2
  796.9 12.7 copy-start.5
  1185.8 13.1 copy-start.3
  1185.8 13.1 copy-start.7
  1553.2 12.6 copy-start.4
  1553.2 12.6 copy-start.6
where the time goes:
time: 1610 us; the launch traced here: 1590 us
  local copies, waits for them, and re-layouts  790 us (49%)
  blocking collectives  304 us (19%)
  matrix products  230 us (14%)
  other arithmetic  168 us (10%)
  waiting for transfers between devices  92.6 us (6%)
    all_to_all x3, blocking collectives, regroup(): lax.all_to_all(halves, axis_name, split_dim + 1, concat_dim + 1, tiled=True)  304 us
    unnamed x32, local copies, waits for them, and re-layouts  269 us
    all_to_all x5, local copies, waits for them, and re-layouts, regroup(): lax.all_to_all(halves, axis_name, split_dim + 1, concat_dim + 1, tiled=True)  165 us
    another operation x4, local copies, waits for them, and re-layouts, regroup(): halves = jnp.stack([jnp.real(volume), jnp.imag(volume)])  122 us
    all_to_all x4, other arithmetic, regroup(): lax.all_to_all(halves, axis_name, split_dim + 1, concat_dim + 1, tiled=True)  120 us
    squeeze x8, local copies, waits for them, and re-layouts, regroup(): return lax.complex(arrived[0], arrived[1])  117 us
    slice x8, local copies, waits for them, and re-layouts, regroup(): return lax.complex(arrived[0], arrived[1])  116 us
    all_to_all x1, waiting for transfers between devices, regroup(): lax.all_to_all(halves, axis_name, split_dim + 1, concat_dim + 1, tiled=True)  92.6 us
  transfers between devices with their start and end apart: 1, of which 1 were waited for; matrix products, arithmetic and copies ran while one was open for 0% of the time, Pallas kernels for 0%

commit v1 on v0

v1 whole, which is shorter than its diff:
```python
import functools

import jax
import jax.numpy as jnp
import ml_dtypes
import numpy as np
from jax import lax
from jax.experimental import pallas as pl
from jax.experimental.pallas import tpu as pltpu
from jax.sharding import PartitionSpec as P

MESH = pl.DeviceIdType.MESH
F32, BF16 = jnp.float32, jnp.bfloat16
N = 64
FIELDS = 32
FG = 4
NG = FIELDS // FG
NU = NG * 4
NPY, NPZ = 4, 2
LAG3, LAG4 = 2, 4
LAG5 = LAG4 + 5
RING = 8
RA = 3


def dft(sign):
    jk = np.outer(np.arange(N), np.arange(N)) % N
    c, s = np.cos(2 * np.pi * jk / N) / 8, sign * np.sin(2 * np.pi * jk / N) / 8
    return np.stack([np.stack([c, -s], 1), np.stack([s, c], 1)])


def split_np(w):
    w = np.asarray(w, np.float32)
    parts = []
    for _ in range(3):
        part = w.astype(ml_dtypes.bfloat16)
        parts.append(part)
        w = w - part.astype(np.float32)
    return np.stack(parts)


def tables():
    fwd, inv = dft(-1), dft(1)
    i16, i32 = np.arange(16), np.arange(32)
    w1, w2, w3, w3i, w4, w5 = [], [], [], [], [], []
    for a in range(NPY):
        to = [16 * ((a + r) % 4) + i16 for r in range(4)]
        frm = [16 * ((a - r) % 4) + i16 for r in range(4)]
        out = np.stack([fwd[:, k] for k in to]).reshape(4, 2, 4, 4, 2, N)
        w1.append(out.transpose(4, 5, 0, 2, 3, 1).reshape(128, 128))
        inn = np.stack([inv[:, :, :, k] for k in frm]).reshape(4, 2, N, 2, 4, 4)
        w5.append(inn.transpose(4, 0, 5, 3, 1, 2).reshape(128, 128))
        for b in range(NPZ):
            half = [32 * (b ^ q) + i32 for q in range(2)]
            m = np.stack([fwd[:, k] for k in half])
            m = np.stack([m[..., y] for y in frm])
            w2.append(m.transpose(1, 2, 3, 0, 4, 5).reshape(128, 128))
            m = np.stack([inv[:, y] for y in to])
            m = np.stack([m[..., k] for k in half])
            w4.append(m.transpose(1, 2, 3, 0, 4, 5).reshape(128, 128))
    for b in range(NPZ):
        half = [32 * (b ^ q) + i32 for q in range(2)]
        m = np.stack([fwd[..., z] for z in half])
        w3.append(m.transpose(0, 3, 4, 1, 2).reshape(128, 128))
        m = np.stack([inv[:, z] for z in half])
        w3i.append(m.transpose(3, 4, 0, 1, 2).reshape(128, 128))
    return [np.stack([split_np(w) for w in ws]) for ws in (w1, w2, w3, w3i, w4, w5)]


def split3(x):
    hi = x.astype(BF16)
    rest = x - hi.astype(F32)
    mid = rest.astype(BF16)
    return hi, mid, (rest - mid.astype(F32)).astype(BF16)


def dot(a, b):
    return jnp.dot(a, b, preferred_element_type=F32)


def left(w, x):
    hi, mid, lo = split3(x)
    wide = dot(w[0][...], jnp.concatenate([hi, mid], 0))
    return wide[:128] + (wide[128:] + dot(w[1][...], jnp.concatenate([hi, lo], 0)))


def right(x, w):
    hi, mid, lo = split3(x)
    wide = dot(jnp.concatenate([hi, mid], 1), w[0][...])
    return wide[:, :128] + (wide[:, 128:] + dot(jnp.concatenate([hi, lo], 1), w[1][...]))


def swap_lanes(tiles):
    lane = lax.broadcasted_iota(jnp.int32, tiles[0].shape, 1)
    odd, high = (lane // 32) % 2 == 1, lane >= 64
    t = list(tiles)
    for lo in (0, 2):
        a, b = t[lo], t[lo + 1]
        t[lo] = jnp.where(odd, pltpu.roll(b, 32, 1), a)
        t[lo + 1] = jnp.where(odd, b, pltpu.roll(a, 96, 1))
    for lo in (0, 1):
        a, b = t[lo], t[lo + 2]
        t[lo] = jnp.where(high, pltpu.roll(b, 64, 1), a)
        t[lo + 2] = jnp.where(high, b, pltpu.roll(a, 64, 1))
    return t


def kernel(rho_re, rho_im, g_re, g_im, t1, t2, t3, t3i, t4, t5, phi_re, phi_im, hat_re, hat_im,
           rin, wraw, wbig, wsmall, ga, gb, a_send, a_recv, b_send, b_recv, c_send, c_recv, d_send, d_recv,
           hat_st, phi_st,
           in_sem, w_sem, hat_sem, phi_sem, as_sem, ar_sem, bs_sem, br_sem, cs_sem, cr_sem, ds_sem, dr_sem):
    me, mz = lax.axis_index("py"), lax.axis_index("pz")
    zero = lax.axis_index("dp")

    def py_peer(r):
        return (zero, mz, lax.rem(me + r, NPY))

    pz_peer = (zero, 1 - mz, me)

    def load_in(g):
        slot = lax.rem(g, 2)
        return [pltpu.make_async_copy(src.at[pl.ds(g * FG, FG)], rin.at[slot, i], in_sem.at[slot, i])
                for i, src in enumerate((rho_re, rho_im))]

    both = me * NPZ + mz
    tabs = [pltpu.make_async_copy(t.at[i], wraw.at[k], w_sem.at[k])
            for k, (t, i) in enumerate(((t1, me), (t2, both), (t3, mz), (t3i, mz), (t4, both), (t5, me)))]
    for cp in load_in(0):
        cp.start()
    for cp in tabs:
        cp.start()
    for cp in load_in(1):
        cp.start()
    barrier = pltpu.get_barrier_semaphore()
    for peer in [py_peer(r) for r in (1, 2, 3)] + [pz_peer]:
        pl.semaphore_signal(barrier, inc=1, device_id=peer, device_id_type=MESH)
    for k, cp in enumerate(tabs):
        cp.wait()
        w1, w2, w3 = (wraw[k, i] for i in range(3))
        if k in (1, 4):
            wbig[k] = jnp.concatenate([jnp.concatenate([w1, w1], 1), jnp.concatenate([w2, w2], 1)], 0)
            wsmall[k] = jnp.concatenate([w3, w1], 1).reshape(wsmall.shape[1:])
        else:
            wbig[k] = jnp.concatenate([jnp.concatenate([w1, w2], 1)] * 2, 0)
            wsmall[k] = jnp.concatenate([w3, w1], 1)
    gr, gi = g_re[...].reshape(512, N), g_im[...].reshape(512, N)
    ga[...] = jnp.concatenate([gr, gr], 1)
    gb[...] = jnp.concatenate([-gi, gi], 1)
    pl.semaphore_wait(barrier, 4)

    def lmat(k):
        return wbig.at[k], wsmall.at[k]

    def rmat(k):
        def small():
            w = wsmall[k]
            return jnp.concatenate([w[:, :128], w[:, 128:]], 0)
        return wbig[k], small()

    def stage1(g, y0, ny):
        slot, ring = lax.rem(g, 2), lax.rem(g, RA)
        w = rmat(0)
        for i in range(ny):
            y = y0 + i
            x = jnp.concatenate([rin[slot, 0, :, y].reshape(128, N), rin[slot, 1, :, y].reshape(128, N)], 1)
            out = right(x, w).T
            rows = pl.ds(pl.multiple_of(y * 8, 8), 8)
            for c in range(4):
                for r in range(4):
                    tile = out[(r * 4 + c) * 8:(r * 4 + c + 1) * 8]
                    if r == 0:
                        a_recv[g * 4 + c, 0, rows, :] = tile
                    else:
                        a_send[ring, c, r - 1, rows, :] = tile

    def a_copy(u, r):
        g, c = u // 4, lax.rem(u, 4)
        ring = lax.rem(g, RA)
        return pltpu.make_async_remote_copy(
            src_ref=a_send.at[ring, c, r - 1], dst_ref=a_recv.at[u, r], send_sem=as_sem.at[ring, c, r - 1],
            recv_sem=ar_sem.at[u, r - 1], device_id=py_peer(r), device_id_type=MESH)

    def b_copy(u):
        ring = lax.rem(u, RING)
        return pltpu.make_async_remote_copy(
            src_ref=b_send.at[ring], dst_ref=b_recv.at[u, 1], send_sem=bs_sem.at[ring], recv_sem=br_sem.at[u],
            device_id=pz_peer, device_id_type=MESH)

    def c_copy(u):
        ring = lax.rem(u, RING)
        return pltpu.make_async_remote_copy(
            src_ref=c_send.at[ring], dst_ref=c_recv.at[u, 1], send_sem=cs_sem.at[ring], recv_sem=cr_sem.at[u],
            device_id=pz_peer, device_id_type=MESH)

    def d_copy(u, r):
        ring = lax.rem(u, RING)
        return pltpu.make_async_remote_copy(
            src_ref=d_send.at[ring, r - 1], dst_ref=d_recv.at[u, r], send_sem=ds_sem.at[ring, r - 1],
            recv_sem=dr_sem.at[u, r - 1], device_id=py_peer(r), device_id_type=MESH)

    def send_a(g):
        for c in range(4):
            for r in (2, 1, 3):
                a_copy(g * 4 + c, r).start()

    def stage2(u):
        for r in (1, 2, 3):
            a_copy(u, r).wait_recv()
        ring = lax.rem(u, RING)

        @pl.when(u >= RING)
        def _():
            b_copy(u - RING).wait_send()

        w = lmat(1)
        for kp in range(2):
            cols = [jnp.concatenate([a_recv[u, r, pl.ds(kk * 2 + ri, 16, stride=8), :]
                                     for r in range(4) for ri in range(2)], 0) for kk in (2 * kp, 2 * kp + 1)]
            out = left(w, jnp.concatenate(cols, 1))
            for i in range(2):
                kk = 2 * kp + i
                b_recv[u, 0, kk] = out[:64, i * 128:(i + 1) * 128]
                b_send[ring, kk] = out[64:, i * 128:(i + 1) * 128]
        b_copy(u).start()

    def hat_copy(u, i):
        slot = lax.rem(u, 2)
        g, c = u // 4, lax.rem(u, 4)
        return pltpu.make_async_copy(
            hat_st.at[slot, i], (hat_re, hat_im)[i].at[pl.ds(g * FG, FG), pl.ds(c * 4, 4)], hat_sem.at[slot, i])

    def stage3(u):
        b_copy(u).wait_recv()
        ring, slot = lax.rem(u, RING), lax.rem(u, 2)
        c = lax.rem(u, 4)

        @pl.when(u >= RING)
        def _():
            c_copy(u - RING).wait_send()

        @pl.when(u >= 2)
        def _():
            for i in range(2):
                hat_copy(u - 2, i).wait()

        wf, wi = rmat(2), rmat(3)
        for kp in range(2):
            rows = []
            for kk in (2 * kp, 2 * kp + 1):
                rows += swap_lanes([b_recv[u, q, kk, ri * 32:(ri + 1) * 32, :] for q in range(2) for ri in range(2)])
            spec = right(jnp.concatenate(rows, 0), wf)
            hats = []
            for i in range(2):
                kk = 2 * kp + i
                gr = pl.ds(pl.multiple_of((c * 4 + kk) * 32, 32), 32)
                gan, gbn = ga[gr, :], gb[gr, :]
                for f in range(FG):
                    s = spec[(i * FG + f) * 32:(i * FG + f + 1) * 32]
                    h = s * gan + pltpu.roll(s, 64, 1) * gbn
                    hat_st[slot, 0, f, kk] = h[:, :N]
                    hat_st[slot, 1, f, kk] = h[:, N:]
                    hats.append(h)
            back = right(jnp.concatenate(hats, 0), wi)
            for i in range(2):
                kk = 2 * kp + i
                t = swap_lanes([back[(i * FG + f) * 32:(i * FG + f + 1) * 32] for f in range(FG)])
                for ri in range(2):
                    c_recv[u, 0, kk, ri * 32:(ri + 1) * 32, :] = t[ri]
                    c_send[ring, kk, ri * 32:(ri + 1) * 32, :] = t[2 + ri]
        c_copy(u).start()
        for i in range(2):
            hat_copy(u, i).start()

    def stage4(u):
        c_copy(u).wait_recv()
        ring = lax.rem(u, RING)

        @pl.when(u >= RING)
        def _():
            for r in (1, 2, 3):
                d_copy(u - RING, r).wait_send()

        w = lmat(4)
        for kp in range(2):
            cols = [jnp.concatenate([c_recv[u, q, kk] for q in range(2)], 0) for kk in (2 * kp, 2 * kp + 1)]
            out = left(w, jnp.concatenate(cols, 1))
            for i in range(2):
                kk = 2 * kp + i
                for r in range(4):
                    for ro in range(2):
                        rows = pl.ds(kk * 2 + ro, 16, stride=8)
                        tile = out[(r * 2 + ro) * 16:(r * 2 + ro + 1) * 16, i * 128:(i + 1) * 128]
                        if r == 0:
                            d_recv[u, 0, rows, :] = tile
                        else:
                            d_send[ring, r - 1, rows, :] = tile
        for r in (2, 1, 3):
            d_copy(u, r).start()

    def phi_copy(g, i):
        slot = lax.rem(g, 2)
        return pltpu.make_async_copy(phi_st.at[slot, i], (phi_re, phi_im)[i].at[pl.ds(g * FG, FG)],
                                     phi_sem.at[slot, i])

    def stage5(g, y0, ny):
        slot = lax.rem(g, 2)
        w = rmat(5)
        for i in range(ny):
            y = y0 + i
            rows = pl.ds(pl.multiple_of(y * 8, 8), 8)
            x = jnp.concatenate([d_recv[g * 4 + c, r, rows, :] for c in range(4) for r in range(4)], 0)
            out = right(x.T, w)
            phi_st[slot, 0, :, y] = out[:, :N].reshape(FG, 32, N)
            phi_st[slot, 1, :, y] = out[:, N:].reshape(FG, 32, N)

    for g in range(2):
        for cp in load_in(g):
            cp.wait()

        @pl.loop(0, 4)
        def _(q, g=g):
            stage1(g, q * 4, 4)

        send_a(g)
        for cp in load_in(g + 2):
            cp.start()

    def step(t, carry):
        c = lax.rem(t, 4)
        g1 = t // 4 + 2

        @pl.when(t < NU)
        def _():
            stage2(t)

        u3 = t - LAG3

        @pl.when(jnp.logical_and(u3 >= 0, u3 < NU))
        def _():
            stage3(u3)

        u4 = t - LAG4

        @pl.when(jnp.logical_and(u4 >= 0, u4 < NU))
        def _():
            stage4(u4)

        @pl.when(g1 < NG)
        def _():
            @pl.when(c == 0)
            def _():
                for cp in load_in(g1):
                    cp.wait()

                @pl.when(g1 >= RA)
                def _():
                    for cc in range(4):
                        for r in (1, 2, 3):
                            a_copy((g1 - RA) * 4 + cc, r).wait_send()

            stage1(g1, c * 4, 4)

            @pl.when(c == 3)
            def _():
                send_a(g1)

                @pl.when(g1 + 2 < NG)
                def _():
                    for cp in load_in(g1 + 2):
                        cp.start()

        u5 = t - LAG5
        g5 = u5 // 4
        c5 = lax.rem(u5 + 16, 4)

        @pl.when(u5 >= 0)
        def _():
            @pl.when(c5 == 0)
            def _():
                for cc in range(4):
                    for r in (1, 2, 3):
                        d_copy(g5 * 4 + cc, r).wait_recv()

                @pl.when(g5 >= 2)
                def _():
                    for i in range(2):
                        phi_copy(g5 - 2, i).wait()

            stage5(g5, c5 * 4, 4)

            @pl.when(c5 == 3)
            def _():
                for i in range(2):
                    phi_copy(g5, i).start()

        return carry

    lax.fori_loop(0, NU + LAG5, step, 0)

    for g in range(NG - 2, NG):
        for i in range(2):
            phi_copy(g, i).wait()
    for u in range(NU - 2, NU):
        for i in range(2):
            hat_copy(u, i).wait()
    for g in range(NG - RA, NG):
        for c in range(4):
            for r in (1, 2, 3):
                a_copy(g * 4 + c, r).wait_send()
    for u in range(NU - RING, NU):
        b_copy(u).wait_send()
        c_copy(u).wait_send()
        for r in (1, 2, 3):
            d_copy(u, r).wait_send()


def solution(mesh):
    consts = tables()

    def local_solve(rho_re, rho_im, g_re, g_im):
        dma, vmem, hbm = pltpu.SemaphoreType.DMA, pltpu.VMEM, pl.BlockSpec(memory_space=pl.ANY)
        tabs = [jnp.asarray(c) for c in consts]
        field = jax.ShapeDtypeStruct((FIELDS, 16, 32, N), F32)
        outs = pl.pallas_call(
            kernel,
            out_shape=[field] * 4,
            in_specs=[hbm, hbm] + [pl.BlockSpec(memory_space=pltpu.VMEM)] * 2 + [hbm] * 6,
            out_specs=[hbm] * 4,
            scratch_shapes=[
                vmem((2, 2, FG, 16, 32, N), F32),
                vmem((6, 3, 128, 128), BF16),
                vmem((6, 256, 256), BF16),
                vmem((6, 128, 256), BF16),
                vmem((512, 128), F32), vmem((512, 128), F32),
                vmem((RA, 4, 3, 128, 128), F32),
                vmem((NU, 4, 128, 128), F32),
                vmem((RING, 4, 64, 128), F32),
                vmem((NU, 2, 4, 64, 128), F32),
                vmem((RING, 4, 64, 128), F32),
                vmem((NU, 2, 4, 64, 128), F32),
                vmem((RING, 3, 128, 128), F32),
                vmem((NU, 4, 128, 128), F32),
                vmem((2, 2, FG, 4, 32, N), F32),
                vmem((2, 2, FG, 16, 32, N), F32),
                dma((2, 2)), dma((6,)), dma((2, 2)), dma((2, 2)),
                dma((RA, 4, 3)), dma((NU, 3)), dma((RING,)), dma((NU,)), dma((RING,)), dma((NU,)),
                dma((RING, 3)), dma((NU, 3)),
            ],
            compiler_params=pltpu.CompilerParams(collective_id=0, has_side_effects=True,
                                                 vmem_limit_bytes=60 * 2 ** 20),
            name="spectral",
        )(jnp.transpose(rho_re, (0, 2, 3, 1)), jnp.transpose(rho_im, (0, 2, 3, 1)), g_re, g_im, *tabs)
        phi_re, phi_im, hat_re, hat_im = outs
        return jnp.transpose(phi_re, (0, 3, 1, 2)), jnp.transpose(phi_im, (0, 3, 1, 2)), hat_re, hat_im

    space_layout = P("dp", None, "py", "pz")
    wave_layout = P("dp", "py", "pz", None)
    green_layout = P("py", "pz", None)
    return jax.shard_map(local_solve, mesh=mesh,
                         in_specs=(space_layout, space_layout, green_layout, green_layout),
                         out_specs=(space_layout, space_layout, wave_layout, wave_layout),
                         check_vma=False)
```

time: 1610 us -> 232 us (0.14); the launches traced: 1590 us -> 232 us
  local copies, waits for them, and re-layouts: 790 us -> 25.8 us
  blocking collectives: 304 us -> 0 us
  matrix products: 230 us -> 0 us
  Pallas kernels: 0 us -> 205 us
  other arithmetic: 168 us -> 0.01 us
  waiting for transfers between devices: 92.6 us -> 0 us
    all_to_all x3 -> x0, blocking collectives: 304 us -> none  [regroup(): lax.all_to_all(halves, axis_name, split_dim + 1, concat_dim + 1, tiled=True)]
    unnamed x32 -> x10, local copies, waits for them, and re-layouts: 269 us -> 25.8 us
    another operation x18 -> x0, matrix products: 230 us -> none  [the longest x3 40.6 us: local_solve(): jnp.fft.fft(volume, axis=3, norm='ortho') * lax.complex(g_re, g_im)]
    pallas_call x0 -> x1, Pallas kernels: none -> 205 us  [local_solve(): pl.pallas_call(kernel, out_shape=[field] * 4, in_specs=[hbm, hbm] + [pl.B...]
    all_to_all x5 -> x0, local copies, waits for them, and re-layouts: 165 us -> none  [regroup(): lax.all_to_all(halves, axis_name, split_dim + 1, concat_dim + 1, tiled=True)]
    another operation x4 -> x0, local copies, waits for them, and re-layouts: 122 us -> none  [regroup(): halves = jnp.stack([jnp.real(volume), jnp.imag(volume)])]
    all_to_all x4 -> x0, other arithmetic: 120 us -> none  [regroup(): lax.all_to_all(halves, axis_name, split_dim + 1, concat_dim + 1, tiled=True)]
    squeeze x8 -> x0, local copies, waits for them, and re-layouts: 117 us -> none  [regroup(): return lax.complex(arrived[0], arrived[1])]
  transfers between devices with their start and end apart: 1 -> 0, of which waited for: 1 -> 0; matrix products, arithmetic and copies ran while one was open for 0% -> 0% of each run, Pallas kernels for 0% -> 0%
where the time goes in v1:
time: 232 us
  Pallas kernels  205 us (88%)
  local copies, waits for them, and re-layouts  25.8 us (11%)
    pallas_call x1, Pallas kernels, local_solve(): pl.pallas_call(kernel, out_shape=[field] * 4, in_specs=[hbm, hbm] + [pl.B...  205 us
    unnamed x10, local copies, waits for them, and re-layouts  25.8 us

profile of v1, /device:TPU:0, one launch (start us, length us, event | category | flops | bytes accessed | tf_op | source)
XLA Modules:
  0.0 231.7 jit_solution(7958445605175363974)
XLA Ops:
  0.6 205.2 %spectral.1 = (f32[32,16,32,64]{3,2,1,0:T(8,128)}, f32[32,16,32,64]{3,2,1,0:T(8,128)}, f32[32,16,32,64]{3,2,1,0:T(8,128)}, f32[32,16,32,64]{3,2,1,0:T(8,128)}) custom-call(f32[32,16,32,64]{3,2,1,0:T(8,128)} %bitcast.4, f32[32,16,32,64]{3,2,1,0:T(8,128)} %bitcast.5, f32[16,32,64]{2,1,0:T(8,128)} %g_re.1, f32[16,32,64]{2,1,0:T(8,128)} %g_im.1, ...), custom_call_target="tpu_custom_call" | custom-call | tf_op jit(solution)/shard_map/spectral/pallas_call | solution.py:424
  205.8 8.4 %copy.18 = f32[32,64,16,32]{1,3,2,0:T(8,128)} copy(f32[32,64,16,32]{1,3,2,0:T(8,128)} %bitcast.9) | data formatting | bytes 8388608
  214.2 0.0 copy-start
  214.2 0.0 slice-start
  214.2 8.9 %copy.19 = f32[32,64,16,32]{1,3,2,0:T(8,128)} copy(f32[32,64,16,32]{1,3,2,0:T(8,128)} %bitcast.8) | data formatting | bytes 8388608
  223.1 0.0 copy-done
  223.1 0.0 slice-start.1
  223.1 4.2 %copy.20 = f32[32,16,32,64]{3,2,1,0:T(8,128)} copy(f32[32,16,32,64]{3,2,1,0:T(8,128)S(1)} %copy-done) | data formatting | bytes 8388608
  227.3 0.0 slice-done
  227.3 0.9 slice-done.1
  228.3 3.4 %copy.21 = f32[32,16,32,64]{3,2,1,0:T(8,128)} copy(f32[32,16,32,64]{3,2,1,0:T(8,128)S(1)} %bitcast.7) | data formatting | bytes 8388608
  (1 shorter events, 0.0 us)
Async XLA Ops:
  214.2 8.9 %copy-start = (f32[32,16,32,64]{3,2,1,0:T(8,128)S(1)}, f32[32,16,32,64]{3,2,1,0:T(8,128)}, u32[]{:S(2)}) copy-start(f32[32,16,32,64]{3,2,1,0:T(8,128)} %get-tuple-element.18) | copy-start | bytes 12582916
  214.2 13.1 %slice-start = ((s8[8388608]{0:T(1024)(128)(4,1)}), s8[4194304]{0:T(1024)(128)(4,1)S(1)}, s32[]{:S(2)}) async-start(s8[8388608]{0:T(1024)(128)(4,1)} %bitcast.6), calls=%async_computation | async-start | bytes 8388608
  223.1 5.2 %slice-start.1 = ((s8[8388608]{0:T(1024)(128)(4,1)}), s8[4194304]{0:T(1024)(128)(4,1)S(1)}, s32[]{:S(2)}) async-start(s8[8388608]{0:T(1024)(128)(4,1)} %bitcast.6), calls=%async_computation.1 | async-start | bytes 8388608

commit v2 on v1

--- a/solution.py
+++ b/solution.py
@@ -21,6 +21,7 @@
 LAG5 = LAG4 + 5
 RING = 8
 RA = 3
+FB, SLOTS = 2, 4
 
 
 def dft(sign):
@@ -105,10 +106,9 @@
     return t
 
 
-def kernel(rho_re, rho_im, g_re, g_im, t1, t2, t3, t3i, t4, t5, phi_re, phi_im, hat_re, hat_im,
-           rin, wraw, wbig, wsmall, ga, gb, a_send, a_recv, b_send, b_recv, c_send, c_recv, d_send, d_recv,
-           hat_st, phi_st,
-           in_sem, w_sem, hat_sem, phi_sem, as_sem, ar_sem, bs_sem, br_sem, cs_sem, cr_sem, ds_sem, dr_sem):
+def kernel(rho_re, rho_im, g_re, g_im, t1, t2, t3, t3i, t4, t5, d_recv, hat,
+           rin, wraw, wbig, wsmall, ga, gb, a_send, a_recv, b_send, b_recv, c_send, c_recv, d_send,
+           in_sem, w_sem, as_sem, ar_sem, bs_sem, br_sem, cs_sem, cr_sem, ds_sem, dr_sem):
     me, mz = lax.axis_index("py"), lax.axis_index("pz")
     zero = lax.axis_index("dp")
 
@@ -223,25 +223,13 @@
                 b_send[ring, kk] = out[64:, i * 128:(i + 1) * 128]
         b_copy(u).start()
 
-    def hat_copy(u, i):
-        slot = lax.rem(u, 2)
-        g, c = u // 4, lax.rem(u, 4)
-        return pltpu.make_async_copy(
-            hat_st.at[slot, i], (hat_re, hat_im)[i].at[pl.ds(g * FG, FG), pl.ds(c * 4, 4)], hat_sem.at[slot, i])
-
     def stage3(u):
         b_copy(u).wait_recv()
-        ring, slot = lax.rem(u, RING), lax.rem(u, 2)
-        c = lax.rem(u, 4)
+        ring, c, f0 = lax.rem(u, RING), lax.rem(u, 4), u // 4 * FG
 
         @pl.when(u >= RING)
         def _():
             c_copy(u - RING).wait_send()
-
-        @pl.when(u >= 2)
-        def _():
-            for i in range(2):
-                hat_copy(u - 2, i).wait()
 
         wf, wi = rmat(2), rmat(3)
         for kp in range(2):
@@ -257,8 +245,7 @@
                 for f in range(FG):
                     s = spec[(i * FG + f) * 32:(i * FG + f + 1) * 32]
                     h = s * gan + pltpu.roll(s, 64, 1) * gbn
-                    hat_st[slot, 0, f, kk] = h[:, :N]
-                    hat_st[slot, 1, f, kk] = h[:, N:]
+                    hat[f0 + f, c * 4 + kk] = h
                     hats.append(h)
             back = right(jnp.concatenate(hats, 0), wi)
             for i in range(2):
@@ -268,8 +255,6 @@
                     c_recv[u, 0, kk, ri * 32:(ri + 1) * 32, :] = t[ri]
                     c_send[ring, kk, ri * 32:(ri + 1) * 32, :] = t[2 + ri]
         c_copy(u).start()
-        for i in range(2):
-            hat_copy(u, i).start()
 
     def stage4(u):
         c_copy(u).wait_recv()
@@ -297,21 +282,16 @@
         for r in (2, 1, 3):
             d_copy(u, r).start()
 
-    def phi_copy(g, i):
-        slot = lax.rem(g, 2)
-        return pltpu.make_async_copy(phi_st.at[slot, i], (phi_re, phi_im)[i].at[pl.ds(g * FG, FG)],
-                                     phi_sem.at[slot, i])
-
     def stage5(g, y0, ny):
-        slot = lax.rem(g, 2)
         w = rmat(5)
         for i in range(ny):
             y = y0 + i
             rows = pl.ds(pl.multiple_of(y * 8, 8), 8)
             x = jnp.concatenate([d_recv[g * 4 + c, r, rows, :] for c in range(4) for r in range(4)], 0)
             out = right(x.T, w)
-            phi_st[slot, 0, :, y] = out[:, :N].reshape(FG, 32, N)
-            phi_st[slot, 1, :, y] = out[:, N:].reshape(FG, 32, N)
+            for f in range(FG):
+                for r in range(4):
+                    d_recv[g * 4 + f, r, rows, :] = out[(f * 4 + r) * 8:(f * 4 + r + 1) * 8]
 
     for g in range(2):
         for cp in load_in(g):
@@ -381,28 +361,12 @@
                     for r in (1, 2, 3):
                         d_copy(g5 * 4 + cc, r).wait_recv()
 
-                @pl.when(g5 >= 2)
-                def _():
-                    for i in range(2):
-                        phi_copy(g5 - 2, i).wait()
-
             stage5(g5, c5 * 4, 4)
 
-            @pl.when(c5 == 3)
-            def _():
-                for i in range(2):
-                    phi_copy(g5, i).start()
-
         return carry
 
     lax.fori_loop(0, NU + LAG5, step, 0)
 
-    for g in range(NG - 2, NG):
-        for i in range(2):
-            phi_copy(g, i).wait()
-    for u in range(NU - 2, NU):
-        for i in range(2):
-            hat_copy(u, i).wait()
     for g in range(NG - RA, NG):
         for c in range(4):
             for r in (1, 2, 3):
@@ -414,6 +378,42 @@
             d_copy(u, r).wait_send()
 
 
+def unpack(phi, hat, phi_re, phi_im, hat_re, hat_im, st, sem):
+    outs = (phi_re, phi_im, hat_re, hat_im)
+
+    def copy(i, k):
+        slot = lax.rem(i, SLOTS)
+        return pltpu.make_async_copy(st.at[slot, k], outs[k].at[pl.ds(i * FB, FB)], sem.at[slot, k])
+
+    def step(i, carry):
+        slot = lax.rem(i, SLOTS)
+
+        @pl.when(i >= SLOTS)
+        def _():
+            for k in range(4):
+                copy(i - SLOTS, k).wait()
+
+        for f in range(FB):
+            h = hat[i * FB + f].reshape(512, 128)
+            st[slot, 2, f] = h[:, :N].reshape(16, 32, N)
+            st[slot, 3, f] = h[:, N:].reshape(16, 32, N)
+        for k in (2, 3):
+            copy(i, k).start()
+        for f in range(FB):
+            for r in range(4):
+                p = phi[i * FB + f, r]
+                st[slot, 0, f, :, r * 8:(r + 1) * 8] = p[:, :N].reshape(16, 8, N)
+                st[slot, 1, f, :, r * 8:(r + 1) * 8] = p[:, N:].reshape(16, 8, N)
+        for k in (0, 1):
+            copy(i, k).start()
+        return carry
+
+    lax.fori_loop(0, FIELDS // FB, step, 0)
+    for i in range(FIELDS // FB - SLOTS, FIELDS // FB):
+        for k in range(4):
+            copy(i, k).wait()
+
+
 def solution(mesh):
     consts = tables()
 
@@ -421,11 +421,11 @@
         dma, vmem, hbm = pltpu.SemaphoreType.DMA, pltpu.VMEM, pl.BlockSpec(memory_space=pl.ANY)
         tabs = [jnp.asarray(c) for c in consts]
         field = jax.ShapeDtypeStruct((FIELDS, 16, 32, N), F32)
-        outs = pl.pallas_call(
+        phi, hat = pl.pallas_call(
             kernel,
-            out_shape=[field] * 4,
+            out_shape=[pltpu.VMEM((NU, 4, 128, 128), F32), pltpu.VMEM((FIELDS, 16, 32, 128), F32)],
             in_specs=[hbm, hbm] + [pl.BlockSpec(memory_space=pltpu.VMEM)] * 2 + [hbm] * 6,
-            out_specs=[hbm] * 4,
+            out_specs=[pl.BlockSpec(memory_space=pltpu.VMEM)] * 2,
             scratch_shapes=[
                 vmem((2, 2, FG, 16, 32, N), F32),
                 vmem((6, 3, 128, 128), BF16),
@@ -439,18 +439,24 @@
                 vmem((RING, 4, 64, 128), F32),
                 vmem((NU, 2, 4, 64, 128), F32),
                 vmem((RING, 3, 128, 128), F32),
-                vmem((NU, 4, 128, 128), F32),
-                vmem((2, 2, FG, 4, 32, N), F32),
-                vmem((2, 2, FG, 16, 32, N), F32),
-                dma((2, 2)), dma((6,)), dma((2, 2)), dma((2, 2)),
+                dma((2, 2)), dma((6,)),
                 dma((RA, 4, 3)), dma((NU, 3)), dma((RING,)), dma((NU,)), dma((RING,)), dma((NU,)),
                 dma((RING, 3)), dma((NU, 3)),
             ],
             compiler_params=pltpu.CompilerParams(collective_id=0, has_side_effects=True,
-                                                 vmem_limit_bytes=60 * 2 ** 20),
+                                                 vmem_limit_bytes=44 * 2 ** 20),
             name="spectral",
         )(jnp.transpose(rho_re, (0, 2, 3, 1)), jnp.transpose(rho_im, (0, 2, 3, 1)), g_re, g_im, *tabs)
-        phi_re, phi_im, hat_re, hat_im = outs
+        phi, hat = (pltpu.with_memory_space_constraint(x, pltpu.VMEM) for x in (phi, hat))
+        phi_re, phi_im, hat_re, hat_im = pl.pallas_call(
+            unpack,
+            out_shape=[field] * 4,
+            in_specs=[pl.BlockSpec(memory_space=pltpu.VMEM)] * 2,
+            out_specs=[hbm] * 4,
+            scratch_shapes=[vmem((SLOTS, 4, FB, 16, 32, N), F32), dma((SLOTS, 4))],
+            compiler_params=pltpu.CompilerParams(vmem_limit_bytes=20 * 2 ** 20),
+            name="unpack",
+        )(phi, hat)
         return jnp.transpose(phi_re, (0, 3, 1, 2)), jnp.transpose(phi_im, (0, 3, 1, 2)), hat_re, hat_im
 
     space_layout = P("dp", None, "py", "pz")

time: 232 us -> 216 us (0.931)
  local copies, waits for them, and re-layouts: 25.8 us -> 0 us
  Pallas kernels: 205 us -> 215 us
    unnamed x10 -> x0, local copies, waits for them, and re-layouts: 25.8 us -> none
    pallas_call x1 -> x2, Pallas kernels: 205 us -> 215 us  [the longest x1 204 us: local_solve(): pl.pallas_call(kernel, out_shape=[pltpu.VMEM((NU, 4, 128, 128), F32), plt...]
where the time goes in v2:
time: 216 us; the launch traced here: 215 us
  Pallas kernels  215 us (100%)
    pallas_call x1, Pallas kernels, local_solve(): pl.pallas_call(kernel, out_shape=[pltpu.VMEM((NU, 4, 128, 128), F32), plt...  204 us
    pallas_call x1, Pallas kernels, local_solve(): pl.pallas_call(unpack, out_shape=[field] * 4, in_specs=[pl.BlockSpec(memo...  11.2 us

profile of v2, /device:TPU:0, one launch (start us, length us, event | category | flops | bytes accessed | tf_op | source)
XLA Modules:
  0.0 215.4 jit_solution(6243331953611478192)
XLA Ops:
  0.6 203.6 %spectral.1 = (f32[32,4,128,128]{3,2,1,0:T(8,128)S(1)}, f32[32,16,32,128]{3,2,1,0:T(8,128)S(1)}) custom-call(f32[32,16,32,64]{3,2,1,0:T(8,128)} %bitcast.4, f32[32,16,32,64]{3,2,1,0:T(8,128)} %bitcast.5, f32[16,32,64]{2,1,0:T(8,128)} %g_re.1, f32[16,32,64]{2,1,0:T(8,128)} %g_im.1, bf16[4,3,128,128]{3,2,1,0:T(8,128)(2,1)} %constant.12.clone.t1, ...), custom_call_target="tpu_custom_call" | custom-call | tf_op jit(solution)/shard_map/spectral/pallas_call | solution.py:424
  204.2 11.2 %unpack.1 = (f32[32,16,32,64]{3,2,1,0:T(8,128)}, f32[32,16,32,64]{3,2,1,0:T(8,128)}, f32[32,16,32,64]{3,2,1,0:T(8,128)}, f32[32,16,32,64]{3,2,1,0:T(8,128)}) custom-call(f32[32,4,128,128]{3,2,1,0:T(8,128)S(1)} %get-tuple-element.10.phi, f32[32,16,32,128]{3,2,1,0:T(8,128)S(1)} %get-tuple-element.11.hat), custom_call_target="tpu_custom_call" | custom-call | tf_op jit(solution)/shard_map/unpack/pallas_call | solution.py:451

commit v3 on v2

--- a/solution.py
+++ b/solution.py
@@ -21,7 +21,7 @@
 LAG5 = LAG4 + 5
 RING = 8
 RA = 3
-FB, SLOTS = 2, 4
+FB, SLOTS = 2, 8
 
 
 def dft(sign):
@@ -91,6 +91,19 @@
     return wide[:, :128] + (wide[:, 128:] + dot(jnp.concatenate([hi, lo], 1), w[1][...]))
 
 
+def left_table(w1, w2, w3):
+    pairs = [jnp.concatenate([a, b], 1) for a, b in ((w1, w1), (w2, w2), (w3, w1))]
+    return jnp.concatenate(pairs[:2], 0), pairs[2]
+
+
+def right_table(w1, w2, w3):
+    return jnp.concatenate([jnp.concatenate([w1, w2], 1)] * 2, 0), jnp.concatenate([w3, w1], 1)
+
+
+def from_wide(w):
+    return jnp.concatenate([w[:, :128], w[:, 128:]], 0)
+
+
 def swap_lanes(tiles):
     lane = lax.broadcasted_iota(jnp.int32, tiles[0].shape, 1)
     odd, high = (lane // 32) % 2 == 1, lane >= 64
@@ -107,8 +120,8 @@
 
 
 def kernel(rho_re, rho_im, g_re, g_im, t1, t2, t3, t3i, t4, t5, d_recv, hat,
-           rin, wraw, wbig, wsmall, ga, gb, a_send, a_recv, b_send, b_recv, c_send, c_recv, d_send,
-           in_sem, w_sem, as_sem, ar_sem, bs_sem, br_sem, cs_sem, cr_sem, ds_sem, dr_sem):
+           rin, gin, wraw, wbig, wsmall, ga, gb, a_send, a_recv, b_send, b_recv, c_send, c_recv, d_send,
+           in_sem, g_sem, w_sem, as_sem, ar_sem, bs_sem, br_sem, cs_sem, cr_sem, ds_sem, dr_sem):
     me, mz = lax.axis_index("py"), lax.axis_index("pz")
     zero = lax.axis_index("dp")
 
@@ -122,40 +135,27 @@
         return [pltpu.make_async_copy(src.at[pl.ds(g * FG, FG)], rin.at[slot, i], in_sem.at[slot, i])
                 for i, src in enumerate((rho_re, rho_im))]
 
+    barrier = pltpu.get_barrier_semaphore()
+    for peer in [py_peer(r) for r in (1, 2, 3)] + [pz_peer]:
+        pl.semaphore_signal(barrier, inc=1, device_id=peer, device_id_type=MESH)
     both = me * NPZ + mz
     tabs = [pltpu.make_async_copy(t.at[i], wraw.at[k], w_sem.at[k])
             for k, (t, i) in enumerate(((t1, me), (t2, both), (t3, mz), (t3i, mz), (t4, both), (t5, me)))]
-    for cp in load_in(0):
+    greens = [pltpu.make_async_copy(src, gin.at[i], g_sem.at[i]) for i, src in enumerate((g_re, g_im))]
+    for cp in tabs[:1] + load_in(0) + tabs[1:] + greens + load_in(1):
         cp.start()
-    for cp in tabs:
-        cp.start()
-    for cp in load_in(1):
-        cp.start()
-    barrier = pltpu.get_barrier_semaphore()
-    for peer in [py_peer(r) for r in (1, 2, 3)] + [pz_peer]:
-        pl.semaphore_signal(barrier, inc=1, device_id=peer, device_id_type=MESH)
-    for k, cp in enumerate(tabs):
-        cp.wait()
-        w1, w2, w3 = (wraw[k, i] for i in range(3))
-        if k in (1, 4):
-            wbig[k] = jnp.concatenate([jnp.concatenate([w1, w1], 1), jnp.concatenate([w2, w2], 1)], 0)
-            wsmall[k] = jnp.concatenate([w3, w1], 1).reshape(wsmall.shape[1:])
-        else:
-            wbig[k] = jnp.concatenate([jnp.concatenate([w1, w2], 1)] * 2, 0)
-            wsmall[k] = jnp.concatenate([w3, w1], 1)
-    gr, gi = g_re[...].reshape(512, N), g_im[...].reshape(512, N)
-    ga[...] = jnp.concatenate([gr, gr], 1)
-    gb[...] = jnp.concatenate([-gi, gi], 1)
-    pl.semaphore_wait(barrier, 4)
+
+    def table(k):
+        tabs[k].wait()
+        wide, narrow = (left_table if k in (1, 4) else right_table)(*(wraw[k, i] for i in range(3)))
+        wbig[k] = wide
+        wsmall[k] = narrow
 
     def lmat(k):
         return wbig.at[k], wsmall.at[k]
 
     def rmat(k):
-        def small():
-            w = wsmall[k]
-            return jnp.concatenate([w[:, :128], w[:, 128:]], 0)
-        return wbig[k], small()
+        return wbig[k], from_wide(wsmall[k])
 
     def stage1(g, y0, ny):
         slot, ring = lax.rem(g, 2), lax.rem(g, RA)
@@ -177,26 +177,42 @@
         g, c = u // 4, lax.rem(u, 4)
         ring = lax.rem(g, RA)
         return pltpu.make_async_remote_copy(
-            src_ref=a_send.at[ring, c, r - 1], dst_ref=a_recv.at[u, r], send_sem=as_sem.at[ring, c, r - 1],
-            recv_sem=ar_sem.at[u, r - 1], device_id=py_peer(r), device_id_type=MESH)
+            src_ref=a_send.at[ring, c, r - 1], dst_ref=a_recv.at[u, r], send_sem=as_sem.at[ring],
+            recv_sem=ar_sem.at[u], device_id=py_peer(r), device_id_type=MESH)
+
+    def a_sent(g):
+        ring = lax.rem(g, RA)
+        return pltpu.make_async_copy(a_send.at[ring], a_send.at[ring], as_sem.at[ring])
+
+    def a_arrived(u):
+        ref = a_recv.at[u, pl.ds(1, 3)]
+        return pltpu.make_async_copy(ref, ref, ar_sem.at[u])
+
+    def d_sent(u):
+        ring = lax.rem(u, RING)
+        return pltpu.make_async_copy(d_send.at[ring], d_send.at[ring], ds_sem.at[ring])
+
+    def d_arrived(g):
+        ref = d_recv.at[pl.ds(g * 4, 4), pl.ds(1, 3)]
+        return pltpu.make_async_copy(ref, ref, dr_sem.at[g])
 
     def b_copy(u):
         ring = lax.rem(u, RING)
         return pltpu.make_async_remote_copy(
-            src_ref=b_send.at[ring], dst_ref=b_recv.at[u, 1], send_sem=bs_sem.at[ring], recv_sem=br_sem.at[u],
+            src_ref=b_send.at[ring], dst_ref=b_recv.at[u, 1], send_sem=bs_sem.at[ring], recv_sem=br_sem.at[ring],
             device_id=pz_peer, device_id_type=MESH)
 
     def c_copy(u):
         ring = lax.rem(u, RING)
         return pltpu.make_async_remote_copy(
-            src_ref=c_send.at[ring], dst_ref=c_recv.at[u, 1], send_sem=cs_sem.at[ring], recv_sem=cr_sem.at[u],
+            src_ref=c_send.at[ring], dst_ref=c_recv.at[u, 1], send_sem=cs_sem.at[ring], recv_sem=cr_sem.at[ring],
             device_id=pz_peer, device_id_type=MESH)
 
     def d_copy(u, r):
         ring = lax.rem(u, RING)
         return pltpu.make_async_remote_copy(
-            src_ref=d_send.at[ring, r - 1], dst_ref=d_recv.at[u, r], send_sem=ds_sem.at[ring, r - 1],
-            recv_sem=dr_sem.at[u, r - 1], device_id=py_peer(r), device_id_type=MESH)
+            src_ref=d_send.at[ring, r - 1], dst_ref=d_recv.at[u, r], send_sem=ds_sem.at[ring],
+            recv_sem=dr_sem.at[u // 4], device_id=py_peer(r), device_id_type=MESH)
 
     def send_a(g):
         for c in range(4):
@@ -204,8 +220,7 @@
                 a_copy(g * 4 + c, r).start()
 
     def stage2(u):
-        for r in (1, 2, 3):
-            a_copy(u, r).wait_recv()
+        a_arrived(u).wait()
         ring = lax.rem(u, RING)
 
         @pl.when(u >= RING)
@@ -262,8 +277,7 @@
 
         @pl.when(u >= RING)
         def _():
-            for r in (1, 2, 3):
-                d_copy(u - RING, r).wait_send()
+            d_sent(u - RING).wait()
 
         w = lmat(4)
         for kp in range(2):
@@ -293,6 +307,7 @@
                 for r in range(4):
                     d_recv[g * 4 + f, r, rows, :] = out[(f * 4 + r) * 8:(f * 4 + r + 1) * 8]
 
+    table(0)
     for g in range(2):
         for cp in load_in(g):
             cp.wait()
@@ -301,9 +316,19 @@
         def _(q, g=g):
             stage1(g, q * 4, 4)
 
+        if g == 0:
+            pl.semaphore_wait(barrier, 4)
         send_a(g)
         for cp in load_in(g + 2):
             cp.start()
+        if g == 0:
+            for k in range(1, 6):
+                table(k)
+            for cp in greens:
+                cp.wait()
+            gr, gi = gin[0].reshape(512, N), gin[1].reshape(512, N)
+            ga[...] = jnp.concatenate([gr, gr], 1)
+            gb[...] = jnp.concatenate([-gi, gi], 1)
 
     def step(t, carry):
         c = lax.rem(t, 4)
@@ -334,9 +359,7 @@
 
                 @pl.when(g1 >= RA)
                 def _():
-                    for cc in range(4):
-                        for r in (1, 2, 3):
-                            a_copy((g1 - RA) * 4 + cc, r).wait_send()
+                    a_sent(g1 - RA).wait()
 
             stage1(g1, c * 4, 4)
 
@@ -357,61 +380,92 @@
         def _():
             @pl.when(c5 == 0)
             def _():
-                for cc in range(4):
-                    for r in (1, 2, 3):
-                        d_copy(g5 * 4 + cc, r).wait_recv()
+                d_arrived(g5).wait()
 
             stage5(g5, c5 * 4, 4)
 
         return carry
 
-    lax.fori_loop(0, NU + LAG5, step, 0)
+    lax.fori_loop(0, NU + LAG4, step, 0)
+    stage5(NG - 2, 12, 4)
+    d_arrived(NG - 1).wait()
 
     for g in range(NG - RA, NG):
-        for c in range(4):
-            for r in (1, 2, 3):
-                a_copy(g * 4 + c, r).wait_send()
+        a_sent(g).wait()
     for u in range(NU - RING, NU):
         b_copy(u).wait_send()
         c_copy(u).wait_send()
-        for r in (1, 2, 3):
-            d_copy(u, r).wait_send()
-
-
-def unpack(phi, hat, phi_re, phi_im, hat_re, hat_im, st, sem):
-    outs = (phi_re, phi_im, hat_re, hat_im)
-
-    def copy(i, k):
+        d_sent(u).wait()
+
+
+def unpack(phi, hat, t5, phi_re, phi_im, hat_re, hat_im, wraw, st, w_sem, sem):
+    tab = pltpu.make_async_copy(t5.at[lax.axis_index("py")], wraw, w_sem)
+    tab.start()
+
+    def copy(outs, n, i, k):
+        return pltpu.make_async_copy(st.at[lax.rem(n, SLOTS), k], outs[k].at[pl.ds(i * FB, FB)],
+                                     sem.at[lax.rem(n, SLOTS), k])
+
+    hats, phis = (hat_re, hat_im), (phi_re, phi_im)
+    jobs = FIELDS // FB
+
+    def free(n):
+        @pl.when(n >= SLOTS)
+        def _():
+            for k in range(2):
+                copy(hats, n - SLOTS, 0, k).wait()
+
+    def hat_job(i, carry):
         slot = lax.rem(i, SLOTS)
-        return pltpu.make_async_copy(st.at[slot, k], outs[k].at[pl.ds(i * FB, FB)], sem.at[slot, k])
-
-    def step(i, carry):
-        slot = lax.rem(i, SLOTS)
-
-        @pl.when(i >= SLOTS)
-        def _():
-            for k in range(4):
-                copy(i - SLOTS, k).wait()
-
+        free(i)
         for f in range(FB):
             h = hat[i * FB + f].reshape(512, 128)
-            st[slot, 2, f] = h[:, :N].reshape(16, 32, N)
-            st[slot, 3, f] = h[:, N:].reshape(16, 32, N)
-        for k in (2, 3):
-            copy(i, k).start()
+            st[slot, 0, f] = h[:, :N].reshape(16, 32, N)
+            st[slot, 1, f] = h[:, N:].reshape(16, 32, N)
+        for k in range(2):
+            copy(hats, i, i, k).start()
+        return carry
+
+    def phi_job(i, carry):
+        n = i + jobs
+        slot = lax.rem(n, SLOTS)
+        free(n)
         for f in range(FB):
             for r in range(4):
                 p = phi[i * FB + f, r]
                 st[slot, 0, f, :, r * 8:(r + 1) * 8] = p[:, :N].reshape(16, 8, N)
                 st[slot, 1, f, :, r * 8:(r + 1) * 8] = p[:, N:].reshape(16, 8, N)
-        for k in (0, 1):
-            copy(i, k).start()
+        for k in range(2):
+            copy(phis, n, i, k).start()
         return carry
 
-    lax.fori_loop(0, FIELDS // FB, step, 0)
-    for i in range(FIELDS // FB - SLOTS, FIELDS // FB):
-        for k in range(4):
-            copy(i, k).wait()
+    last = jobs - FG // FB
+    lax.fori_loop(0, jobs, hat_job, 0)
+    lax.fori_loop(0, last, phi_job, 0)
+    tab.wait()
+    wide, narrow = right_table(*(wraw[i] for i in range(3)))
+    w = wide, from_wide(narrow)
+    for j in range(FG // FB):
+        free(jobs + last + j)
+
+    @pl.loop(0, 4)
+    def _(q):
+        for i in range(4):
+            y = q * 4 + i
+            rows = pl.ds(pl.multiple_of(y * 8, 8), 8)
+            x = jnp.concatenate([phi[NU - 4 + c, r, rows, :] for c in range(4) for r in range(4)], 0)
+            out = right(x.T, w)
+            for f in range(FG):
+                slot = (jobs + last + f // FB) % SLOTS
+                st[slot, 0, f % FB, y] = out[f * 32:(f + 1) * 32, :N]
+                st[slot, 1, f % FB, y] = out[f * 32:(f + 1) * 32, N:]
+
+    for j in range(FG // FB):
+        for k in range(2):
+            copy(phis, jobs + last + j, last + j, k).start()
+    for n in range(2 * jobs - SLOTS, 2 * jobs):
+        for k in range(2):
+            copy(hats, n, 0, k).wait()
 
 
 def solution(mesh):
@@ -424,10 +478,11 @@
         phi, hat = pl.pallas_call(
             kernel,
             out_shape=[pltpu.VMEM((NU, 4, 128, 128), F32), pltpu.VMEM((FIELDS, 16, 32, 128), F32)],
-            in_specs=[hbm, hbm] + [pl.BlockSpec(memory_space=pltpu.VMEM)] * 2 + [hbm] * 6,
+            in_specs=[hbm] * 10,
             out_specs=[pl.BlockSpec(memory_space=pltpu.VMEM)] * 2,
             scratch_shapes=[
                 vmem((2, 2, FG, 16, 32, N), F32),
+                vmem((2, 16, 32, N), F32),
                 vmem((6, 3, 128, 128), BF16),
                 vmem((6, 256, 256), BF16),
                 vmem((6, 128, 256), BF16),
@@ -439,9 +494,8 @@
                 vmem((RING, 4, 64, 128), F32),
                 vmem((NU, 2, 4, 64, 128), F32),
                 vmem((RING, 3, 128, 128), F32),
-                dma((2, 2)), dma((6,)),
-                dma((RA, 4, 3)), dma((NU, 3)), dma((RING,)), dma((NU,)), dma((RING,)), dma((NU,)),
-                dma((RING, 3)), dma((NU, 3)),
+                dma((2, 2)), dma((2,)), dma((6,)), dma((RA,)), dma((NU,)),
+                dma((RING,)), dma((RING,)), dma((RING,)), dma((RING,)), dma((RING,)), dma((NG,)),
             ],
             compiler_params=pltpu.CompilerParams(collective_id=0, has_side_effects=True,
                                                  vmem_limit_bytes=44 * 2 ** 20),
@@ -451,12 +505,12 @@
         phi_re, phi_im, hat_re, hat_im = pl.pallas_call(
             unpack,
             out_shape=[field] * 4,
-            in_specs=[pl.BlockSpec(memory_space=pltpu.VMEM)] * 2,
+            in_specs=[pl.BlockSpec(memory_space=pltpu.VMEM)] * 2 + [hbm],
             out_specs=[hbm] * 4,
-            scratch_shapes=[vmem((SLOTS, 4, FB, 16, 32, N), F32), dma((SLOTS, 4))],
+            scratch_shapes=[vmem((3, 128, 128), BF16), vmem((SLOTS, 2, FB, 16, 32, N), F32), dma, dma((SLOTS, 2))],
             compiler_params=pltpu.CompilerParams(vmem_limit_bytes=20 * 2 ** 20),
             name="unpack",
-        )(phi, hat)
+        )(phi, hat, tabs[5])
         return jnp.transpose(phi_re, (0, 3, 1, 2)), jnp.transpose(phi_im, (0, 3, 1, 2)), hat_re, hat_im
 
     space_layout = P("dp", None, "py", "pz")

time: 216 us -> 211 us (0.977)
  Pallas kernels: 215 us -> 210 us
    pallas_call x1, Pallas kernels: 204 us -> 198 us  [local_solve(): pl.pallas_call(kernel, out_shape=[pltpu.VMEM((NU, 4, 128, 128), F32), plt...]
where the time goes in v3:
time: 211 us
  Pallas kernels  210 us (100%)
    pallas_call x1, Pallas kernels, local_solve(): pl.pallas_call(kernel, out_shape=[pltpu.VMEM((NU, 4, 128, 128), F32), plt...  198 us
    pallas_call x1, Pallas kernels, local_solve(): pl.pallas_call(unpack, out_shape=[field] * 4, in_specs=[pl.BlockSpec(memo...  11.8 us

profile of v3, /device:TPU:0, one launch (start us, length us, event | category | flops | bytes accessed | tf_op | source)
XLA Modules:
  0.0 210.6 jit_solution(3850887185018860355)
XLA Ops:
  0.6 0.0 copy-start
  0.6 198.1 %spectral.1 = (f32[32,4,128,128]{3,2,1,0:T(8,128)S(1)}, f32[32,16,32,128]{3,2,1,0:T(8,128)S(1)}) custom-call(f32[32,16,32,64]{3,2,1,0:T(8,128)} %bitcast.4, f32[32,16,32,64]{3,2,1,0:T(8,128)} %bitcast.5, f32[16,32,64]{2,1,0:T(8,128)} %g_re.1, f32[16,32,64]{2,1,0:T(8,128)} %g_im.1, bf16[4,3,128,128]{3,2,1,0:T(8,128)(2,1)} %constant.12.clone.t1, ...), custom_call_target="tpu_custom_call" | custom-call | tf_op jit(solution)/shard_map/spectral/pallas_call | solution.py:478
  198.8 0.0 copy-done
  198.8 11.8 %unpack.1 = (f32[32,16,32,64]{3,2,1,0:T(8,128)}, f32[32,16,32,64]{3,2,1,0:T(8,128)}, f32[32,16,32,64]{3,2,1,0:T(8,128)}, f32[32,16,32,64]{3,2,1,0:T(8,128)}) custom-call(f32[32,4,128,128]{3,2,1,0:T(8,128)S(1)} %get-tuple-element.10.phi, f32[32,16,32,128]{3,2,1,0:T(8,128)S(1)} %get-tuple-element.11.hat, bf16[4,3,128,128]{3,2,1,0:T(8,128)(2,1)S(1)} %copy-done), custom_call_target="tpu_custom_call" | custom-call | tf_op jit(solution)/shard_map/unpack/pallas_call | solution.py:505
Async XLA Ops:
  0.6 198.1 %copy-start = (bf16[4,3,128,128]{3,2,1,0:T(8,128)(2,1)S(1)}, bf16[4,3,128,128]{3,2,1,0:T(8,128)(2,1)}, u32[]{:S(2)}) copy-start(bf16[4,3,128,128]{3,2,1,0:T(8,128)(2,1)} %constant.17.clone.t5) | copy-start | bytes 1179652

commit v4 on v3

--- a/solution.py
+++ b/solution.py
@@ -19,8 +19,11 @@
 NPY, NPZ = 4, 2
 LAG3, LAG4 = 2, 4
 LAG5 = LAG4 + 5
-RING = 8
+RING = 4
+RECV = 8
 RA = 3
+EARLY = 2
+LATE = 3
 FB, SLOTS = 2, 8
 
 
@@ -121,7 +124,8 @@
 
 def kernel(rho_re, rho_im, g_re, g_im, t1, t2, t3, t3i, t4, t5, d_recv, hat,
            rin, gin, wraw, wbig, wsmall, ga, gb, a_send, a_recv, b_send, b_recv, c_send, c_recv, d_send,
-           in_sem, g_sem, w_sem, as_sem, ar_sem, bs_sem, br_sem, cs_sem, cr_sem, ds_sem, dr_sem):
+           in_sem, first_sem, g_sem, w_sem, as_sem, ar_sem, half_sem, bs_sem, br_sem, cs_sem, cr_sem, part_sem,
+           ds_sem, dr_sem):
     me, mz = lax.axis_index("py"), lax.axis_index("pz")
     zero = lax.axis_index("dp")
 
@@ -135,18 +139,27 @@
         return [pltpu.make_async_copy(src.at[pl.ds(g * FG, FG)], rin.at[slot, i], in_sem.at[slot, i])
                 for i, src in enumerate((rho_re, rho_im))]
 
+    def load_first(q):
+        ys = pl.ds(q * 4, 4)
+        return [pltpu.make_async_copy(src.at[pl.ds(0, FG), ys], rin.at[0, i, :, ys], first_sem.at[q])
+                for i, src in enumerate((rho_re, rho_im))]
+
+    def first_loaded(q):
+        ref = rin.at[0, :, :, pl.ds(q * 4, 4)]
+        return pltpu.make_async_copy(ref, ref, first_sem.at[q])
+
     barrier = pltpu.get_barrier_semaphore()
     for peer in [py_peer(r) for r in (1, 2, 3)] + [pz_peer]:
         pl.semaphore_signal(barrier, inc=1, device_id=peer, device_id_type=MESH)
     both = me * NPZ + mz
-    tabs = [pltpu.make_async_copy(t.at[i], wraw.at[k], w_sem.at[k])
+    tabs = [pltpu.make_async_copy(t.at[i], wraw.at[k], w_sem.at[min(k, 1)])
             for k, (t, i) in enumerate(((t1, me), (t2, both), (t3, mz), (t3i, mz), (t4, both), (t5, me)))]
-    greens = [pltpu.make_async_copy(src, gin.at[i], g_sem.at[i]) for i, src in enumerate((g_re, g_im))]
-    for cp in tabs[:1] + load_in(0) + tabs[1:] + greens + load_in(1):
+    greens = [pltpu.make_async_copy(src, gin.at[i], g_sem) for i, src in enumerate((g_re, g_im))]
+    firsts = [cp for q in range(4) for cp in load_first(q)]
+    for cp in tabs[:1] + firsts + tabs[1:] + greens + load_in(1):
         cp.start()
 
     def table(k):
-        tabs[k].wait()
         wide, narrow = (left_table if k in (1, 4) else right_table)(*(wraw[k, i] for i in range(3)))
         wbig[k] = wide
         wsmall[k] = narrow
@@ -180,6 +193,30 @@
             src_ref=a_send.at[ring, c, r - 1], dst_ref=a_recv.at[u, r], send_sem=as_sem.at[ring],
             recv_sem=ar_sem.at[u], device_id=py_peer(r), device_id_type=MESH)
 
+    def a_half(u, r, h, y0, ny):
+        part = (pl.ds(y0, ny), pl.ds(4 * h, 4))
+        src, dst = (ref.reshape(16, 8, 128).at[part] for ref in (a_send.at[0, u, r - 1], a_recv.at[u, r]))
+        return pltpu.make_async_remote_copy(
+            src_ref=src, dst_ref=dst, send_sem=as_sem.at[0], recv_sem=half_sem.at[u, h],
+            device_id=py_peer(r), device_id_type=MESH)
+
+    def half_arrived(u, h):
+        ref = a_recv.at[u, pl.ds(1, 3), pl.ds(64 * h, 64)]
+        return pltpu.make_async_copy(ref, ref, half_sem.at[u, h])
+
+    def c_part(u, kk):
+        ring = lax.rem(u, RING)
+        return pltpu.make_async_remote_copy(
+            src_ref=c_send.at[ring, kk], dst_ref=c_recv.at[u, 1, kk], send_sem=cs_sem.at[ring],
+            recv_sem=part_sem.at[u - (NU - LATE), kk], device_id=pz_peer, device_id_type=MESH)
+
+    def d_part(u, r, kk):
+        part = (slice(None), pl.ds(2 * kk, 2))
+        src, dst = (ref.reshape(16, 8, 128).at[part] for ref in (d_send.at[u % RING, r - 1], d_recv.at[u, r]))
+        return pltpu.make_async_remote_copy(
+            src_ref=src, dst_ref=dst, send_sem=ds_sem.at[u % RING], recv_sem=dr_sem.at[NG - 1],
+            device_id=py_peer(r), device_id_type=MESH)
+
     def a_sent(g):
         ring = lax.rem(g, RA)
         return pltpu.make_async_copy(a_send.at[ring], a_send.at[ring], as_sem.at[ring])
@@ -199,13 +236,19 @@
     def b_copy(u):
         ring = lax.rem(u, RING)
         return pltpu.make_async_remote_copy(
-            src_ref=b_send.at[ring], dst_ref=b_recv.at[u, 1], send_sem=bs_sem.at[ring], recv_sem=br_sem.at[ring],
+            src_ref=b_send.at[ring], dst_ref=b_recv.at[u, 1], send_sem=bs_sem.at[ring], recv_sem=br_sem.at[lax.rem(u, RECV)],
+            device_id=pz_peer, device_id_type=MESH)
+
+    def b_half(u, h):
+        kk = pl.ds(2 * h, 2)
+        return pltpu.make_async_remote_copy(
+            src_ref=b_send.at[u, kk], dst_ref=b_recv.at[u, 1, kk], send_sem=bs_sem.at[u], recv_sem=br_sem.at[u],
             device_id=pz_peer, device_id_type=MESH)
 
     def c_copy(u):
         ring = lax.rem(u, RING)
         return pltpu.make_async_remote_copy(
-            src_ref=c_send.at[ring], dst_ref=c_recv.at[u, 1], send_sem=cs_sem.at[ring], recv_sem=cr_sem.at[ring],
+            src_ref=c_send.at[ring], dst_ref=c_recv.at[u, 1], send_sem=cs_sem.at[ring], recv_sem=cr_sem.at[lax.rem(u, RECV)],
             device_id=pz_peer, device_id_type=MESH)
 
     def d_copy(u, r):
@@ -219,23 +262,25 @@
             for r in (2, 1, 3):
                 a_copy(g * 4 + c, r).start()
 
+    def y_lines(u, kp):
+        ring = lax.rem(u, RING)
+        cols = [jnp.concatenate([a_recv[u, r, pl.ds(kk * 2 + ri, 16, stride=8), :]
+                                 for r in range(4) for ri in range(2)], 0) for kk in (2 * kp, 2 * kp + 1)]
+        out = left(lmat(1), jnp.concatenate(cols, 1))
+        for i in range(2):
+            kk = 2 * kp + i
+            b_recv[u, 0, kk] = out[:64, i * 128:(i + 1) * 128]
+            b_send[ring, kk] = out[64:, i * 128:(i + 1) * 128]
+
     def stage2(u):
         a_arrived(u).wait()
-        ring = lax.rem(u, RING)
 
         @pl.when(u >= RING)
         def _():
             b_copy(u - RING).wait_send()
 
-        w = lmat(1)
         for kp in range(2):
-            cols = [jnp.concatenate([a_recv[u, r, pl.ds(kk * 2 + ri, 16, stride=8), :]
-                                     for r in range(4) for ri in range(2)], 0) for kk in (2 * kp, 2 * kp + 1)]
-            out = left(w, jnp.concatenate(cols, 1))
-            for i in range(2):
-                kk = 2 * kp + i
-                b_recv[u, 0, kk] = out[:64, i * 128:(i + 1) * 128]
-                b_send[ring, kk] = out[64:, i * 128:(i + 1) * 128]
+            y_lines(u, kp)
         b_copy(u).start()
 
     def stage3(u):
@@ -269,30 +314,39 @@
                 for ri in range(2):
                     c_recv[u, 0, kk, ri * 32:(ri + 1) * 32, :] = t[ri]
                     c_send[ring, kk, ri * 32:(ri + 1) * 32, :] = t[2 + ri]
-        c_copy(u).start()
+
+        @pl.when(u < NU - LATE)
+        def _():
+            c_copy(u).start()
+
+        @pl.when(u >= NU - LATE)
+        def _():
+            for kk in range(4):
+                c_part(u, kk).start()
+
+    def y_lines_back(u, kks):
+        ring = lax.rem(u, RING)
+        cols = [jnp.concatenate([c_recv[u, q, kk] for q in range(2)], 0) for kk in kks]
+        out = left(lmat(4), jnp.concatenate(cols, 1))
+        for i, kk in enumerate(kks):
+            for r in range(4):
+                for ro in range(2):
+                    rows = pl.ds(kk * 2 + ro, 16, stride=8)
+                    tile = out[(r * 2 + ro) * 16:(r * 2 + ro + 1) * 16, i * 128:(i + 1) * 128]
+                    if r == 0:
+                        d_recv[u, 0, rows, :] = tile
+                    else:
+                        d_send[ring, r - 1, rows, :] = tile
 
     def stage4(u):
         c_copy(u).wait_recv()
-        ring = lax.rem(u, RING)
 
         @pl.when(u >= RING)
         def _():
             d_sent(u - RING).wait()
 
-        w = lmat(4)
         for kp in range(2):
-            cols = [jnp.concatenate([c_recv[u, q, kk] for q in range(2)], 0) for kk in (2 * kp, 2 * kp + 1)]
-            out = left(w, jnp.concatenate(cols, 1))
-            for i in range(2):
-                kk = 2 * kp + i
-                for r in range(4):
-                    for ro in range(2):
-                        rows = pl.ds(kk * 2 + ro, 16, stride=8)
-                        tile = out[(r * 2 + ro) * 16:(r * 2 + ro + 1) * 16, i * 128:(i + 1) * 128]
-                        if r == 0:
-                            d_recv[u, 0, rows, :] = tile
-                        else:
-                            d_send[ring, r - 1, rows, :] = tile
+            y_lines_back(u, (2 * kp, 2 * kp + 1))
         for r in (2, 1, 3):
             d_copy(u, r).start()
 
@@ -307,28 +361,54 @@
                 for r in range(4):
                     d_recv[g * 4 + f, r, rows, :] = out[(f * 4 + r) * 8:(f * 4 + r + 1) * 8]
 
+    tabs[0].wait()
     table(0)
-    for g in range(2):
+    for q in range(4):
+        first_loaded(q).wait()
+        stage1(0, q * 4, 4)
+        if q == 0:
+            pl.semaphore_wait(barrier, 4)
+        for r in (2, 1, 3):
+            a_half(0, r, 0, q * 4, 4).start()
+    for u, h in [(0, 1)] + [(u, h) for u in range(1, EARLY) for h in range(2)]:
+        for r in (2, 1, 3):
+            a_half(u, r, h, 0, 16).start()
+    for u in range(EARLY, 4):
+        for r in (2, 1, 3):
+            a_copy(u, r).start()
+    for cp in load_in(2):
+        cp.start()
+    pltpu.make_async_copy(wraw.at[pl.ds(1, 5)], wraw.at[pl.ds(1, 5)], w_sem.at[1]).wait()
+    for k in range(1, 6):
+        table(k)
+    pltpu.make_async_copy(gin, gin, g_sem).wait()
+    gr, gi = gin[0].reshape(512, N), gin[1].reshape(512, N)
+    ga[...] = jnp.concatenate([gr, gr], 1)
+    gb[...] = jnp.concatenate([-gi, gi], 1)
+    for cp in load_in(1):
+        cp.wait()
+
+    @pl.loop(0, 4)
+    def _(q):
+        stage1(1, q * 4, 4)
+
+    send_a(1)
+    for cp in load_in(3):
+        cp.start()
+    for u in range(EARLY):
+        for h in range(2):
+            half_arrived(u, h).wait()
+            y_lines(u, h)
+            b_half(u, h).start()
+    stage3(0)
+
+    def inputs_of(g):
         for cp in load_in(g):
             cp.wait()
 
-        @pl.loop(0, 4)
-        def _(q, g=g):
-            stage1(g, q * 4, 4)
-
-        if g == 0:
-            pl.semaphore_wait(barrier, 4)
-        send_a(g)
-        for cp in load_in(g + 2):
-            cp.start()
-        if g == 0:
-            for k in range(1, 6):
-                table(k)
-            for cp in greens:
-                cp.wait()
-            gr, gi = gin[0].reshape(512, N), gin[1].reshape(512, N)
-            ga[...] = jnp.concatenate([gr, gr], 1)
-            gb[...] = jnp.concatenate([-gi, gi], 1)
+    inputs_of(2)
+    for q in range(EARLY):
+        stage1(2, q * 4, 4)
 
     def step(t, carry):
         c = lax.rem(t, 4)
@@ -340,13 +420,13 @@
 
         u3 = t - LAG3
 
-        @pl.when(jnp.logical_and(u3 >= 0, u3 < NU))
+        @pl.when(u3 >= 1)
         def _():
             stage3(u3)
 
         u4 = t - LAG4
 
-        @pl.when(jnp.logical_and(u4 >= 0, u4 < NU))
+        @pl.when(u4 >= 0)
         def _():
             stage4(u4)
 
@@ -354,8 +434,7 @@
         def _():
             @pl.when(c == 0)
             def _():
-                for cp in load_in(g1):
-                    cp.wait()
+                inputs_of(g1)
 
                 @pl.when(g1 >= RA)
                 def _():
@@ -373,21 +452,35 @@
                         cp.start()
 
         u5 = t - LAG5
-        g5 = u5 // 4
-        c5 = lax.rem(u5 + 16, 4)
 
         @pl.when(u5 >= 0)
         def _():
-            @pl.when(c5 == 0)
+            @pl.when(lax.rem(u5, 4) == 0)
             def _():
-                d_arrived(g5).wait()
-
-            stage5(g5, c5 * 4, 4)
+                d_arrived(u5 // 4).wait()
+
+            stage5(u5 // 4, lax.rem(u5, 4) * 4, 4)
 
         return carry
 
-    lax.fori_loop(0, NU + LAG4, step, 0)
-    stage5(NG - 2, 12, 4)
+    steps = NU - LATE + LAG4
+    lax.fori_loop(EARLY, steps, step, 0)
+    rest = [u5 for u5 in range(steps - LAG5, NU - 4)]
+    u3 = [u for u in range(steps - LAG3, NU)]
+    for u in range(NU - LATE, NU):
+        if u3:
+            stage3(u3.pop(0))
+        d_sent(u - RING).wait()
+        for kk in range(4):
+            c_part(u, kk).wait_recv()
+            y_lines_back(u, (kk,))
+            for r in (2, 1, 3):
+                d_part(u, r, kk).start()
+        for u5 in rest[:2]:
+            if u5 % 4 == 0:
+                d_arrived(u5 // 4).wait()
+            stage5(u5 // 4, u5 % 4 * 4, 4)
+        rest = rest[2:]
     d_arrived(NG - 1).wait()
 
     for g in range(NG - RA, NG):
@@ -398,7 +491,7 @@
         d_sent(u).wait()
 
 
-def unpack(phi, hat, t5, phi_re, phi_im, hat_re, hat_im, wraw, st, w_sem, sem):
+def unpack(phi, hat, t5, phi_re, phi_im, hat_re, hat_im, wraw, st, st_last, w_sem, sem, last_sem):
     tab = pltpu.make_async_copy(t5.at[lax.axis_index("py")], wraw, w_sem)
     tab.start()
 
@@ -439,14 +532,13 @@
             copy(phis, n, i, k).start()
         return carry
 
-    last = jobs - FG // FB
+    def last_copy(k):
+        return pltpu.make_async_copy(st_last.at[k], phis[k].at[pl.ds(FIELDS - FG, FG)], last_sem.at[k])
+
     lax.fori_loop(0, jobs, hat_job, 0)
-    lax.fori_loop(0, last, phi_job, 0)
     tab.wait()
     wide, narrow = right_table(*(wraw[i] for i in range(3)))
     w = wide, from_wide(narrow)
-    for j in range(FG // FB):
-        free(jobs + last + j)
 
     @pl.loop(0, 4)
     def _(q):
@@ -455,15 +547,16 @@
             rows = pl.ds(pl.multiple_of(y * 8, 8), 8)
             x = jnp.concatenate([phi[NU - 4 + c, r, rows, :] for c in range(4) for r in range(4)], 0)
             out = right(x.T, w)
-            for f in range(FG):
-                slot = (jobs + last + f // FB) % SLOTS
-                st[slot, 0, f % FB, y] = out[f * 32:(f + 1) * 32, :N]
-                st[slot, 1, f % FB, y] = out[f * 32:(f + 1) * 32, N:]
-
-    for j in range(FG // FB):
-        for k in range(2):
-            copy(phis, jobs + last + j, last + j, k).start()
-    for n in range(2 * jobs - SLOTS, 2 * jobs):
+            st_last[0, :, y] = out[:, :N].reshape(FG, 32, N)
+            st_last[1, :, y] = out[:, N:].reshape(FG, 32, N)
+
+    for k in range(2):
+        last_copy(k).start()
+    ends = jobs + jobs - FG // FB
+    lax.fori_loop(0, ends - jobs, phi_job, 0)
+    for k in range(2):
+        last_copy(k).wait()
+    for n in range(ends - SLOTS, ends):
         for k in range(2):
             copy(hats, n, 0, k).wait()
 
@@ -494,8 +587,8 @@
                 vmem((RING, 4, 64, 128), F32),
                 vmem((NU, 2, 4, 64, 128), F32),
                 vmem((RING, 3, 128, 128), F32),
-                dma((2, 2)), dma((2,)), dma((6,)), dma((RA,)), dma((NU,)),
-                dma((RING,)), dma((RING,)), dma((RING,)), dma((RING,)), dma((RING,)), dma((NG,)),
+                dma((2, 2)), dma((4,)), dma, dma((2,)), dma((RA,)), dma((NU,)), dma((EARLY, 2)),
+                dma((RING,)), dma((RECV,)), dma((RING,)), dma((RECV,)), dma((LATE, 4)), dma((RING,)), dma((NG,)),
             ],
             compiler_params=pltpu.CompilerParams(collective_id=0, has_side_effects=True,
                                                  vmem_limit_bytes=44 * 2 ** 20),
@@ -507,7 +600,8 @@
             out_shape=[field] * 4,
             in_specs=[pl.BlockSpec(memory_space=pltpu.VMEM)] * 2 + [hbm],
             out_specs=[hbm] * 4,
-            scratch_shapes=[vmem((3, 128, 128), BF16), vmem((SLOTS, 2, FB, 16, 32, N), F32), dma, dma((SLOTS, 2))],
+            scratch_shapes=[vmem((3, 128, 128), BF16), vmem((SLOTS, 2, FB, 16, 32, N), F32),
+                            vmem((2, FG, 16, 32, N), F32), dma, dma((SLOTS, 2)), dma((2,))],
             compiler_params=pltpu.CompilerParams(vmem_limit_bytes=20 * 2 ** 20),
             name="unpack",
         )(phi, hat, tabs[5])

time: 211 us -> 207 us (0.981)
  Pallas kernels: 210 us -> 206 us
    pallas_call x1, Pallas kernels: 198 us -> 194 us  [local_solve(): pl.pallas_call(kernel, out_shape=[pltpu.VMEM((NU, 4, 128, 128), F32), plt...]
where the time goes in v4:
time: 207 us; the launch traced here: 206 us
  Pallas kernels  206 us (100%)
    pallas_call x1, Pallas kernels, local_solve(): pl.pallas_call(kernel, out_shape=[pltpu.VMEM((NU, 4, 128, 128), F32), plt...  194 us
    pallas_call x1, Pallas kernels, local_solve(): pl.pallas_call(unpack, out_shape=[field] * 4, in_specs=[pl.BlockSpec(memo...  11.4 us

profile of v4, /device:TPU:0, one launch (start us, length us, event | category | flops | bytes accessed | tf_op | source)
XLA Modules:
  0.0 206.4 jit_solution(15198490255220020712)
XLA Ops:
  0.6 0.0 copy-start
  0.6 194.3 %spectral.1 = (f32[32,4,128,128]{3,2,1,0:T(8,128)S(1)}, f32[32,16,32,128]{3,2,1,0:T(8,128)S(1)}) custom-call(f32[32,16,32,64]{3,2,1,0:T(8,128)} %bitcast.4, f32[32,16,32,64]{3,2,1,0:T(8,128)} %bitcast.5, f32[16,32,64]{2,1,0:T(8,128)} %g_re.1, f32[16,32,64]{2,1,0:T(8,128)} %g_im.1, bf16[4,3,128,128]{3,2,1,0:T(8,128)(2,1)} %constant.12.clone.t1, ...), custom_call_target="tpu_custom_call" | custom-call | tf_op jit(solution)/shard_map/spectral/pallas_call | solution.py:571
  195.0 0.0 copy-done
  195.0 11.4 %unpack.1 = (f32[32,16,32,64]{3,2,1,0:T(8,128)}, f32[32,16,32,64]{3,2,1,0:T(8,128)}, f32[32,16,32,64]{3,2,1,0:T(8,128)}, f32[32,16,32,64]{3,2,1,0:T(8,128)}) custom-call(f32[32,4,128,128]{3,2,1,0:T(8,128)S(1)} %get-tuple-element.10.phi, f32[32,16,32,128]{3,2,1,0:T(8,128)S(1)} %get-tuple-element.11.hat, bf16[4,3,128,128]{3,2,1,0:T(8,128)(2,1)S(1)} %copy-done), custom_call_target="tpu_custom_call" | custom-call | tf_op jit(solution)/shard_map/unpack/pallas_call | solution.py:598
Async XLA Ops:
  0.6 194.4 %copy-start = (bf16[4,3,128,128]{3,2,1,0:T(8,128)(2,1)S(1)}, bf16[4,3,128,128]{3,2,1,0:T(8,128)(2,1)}, u32[]{:S(2)}) copy-start(bf16[4,3,128,128]{3,2,1,0:T(8,128)(2,1)} %constant.17.clone.t5) | copy-start | bytes 1179652

commit v5 on v4

v5 whole, which is shorter than its diff:
```python
import functools

import jax
import jax.numpy as jnp
import ml_dtypes
import numpy as np
from jax import lax
from jax.experimental import pallas as pl
from jax.experimental.pallas import tpu as pltpu
from jax.sharding import PartitionSpec as P

MESH = pl.DeviceIdType.MESH
L, H, Z, Y, S, Q = 128, 64, 32, 16, 8, 4
F32, BF16 = jnp.float32, jnp.bfloat16
N = 64
FIELDS = 32
FG = 4
NG = FIELDS // FG
NU = NG * 4
NPY, NPZ = 4, 2
LAG3, LAG4 = 2, 4
LAG5 = LAG4 + 5
RING = 4
RECV = 6
RG = 4
RA = 3
AR = 16
EARLY = 2
LATE = 3
FB, SLOTS = 4, 4
HB = 8


def dft(sign):
    jk = np.outer(np.arange(N), np.arange(N)) % N
    c, s = np.cos(2 * np.pi * jk / N) / S, sign * np.sin(2 * np.pi * jk / N) / S
    return np.stack([np.stack([c, -s], 1), np.stack([s, c], 1)])


def split_np(w):
    w = np.asarray(w, np.float32)
    parts = []
    for _ in range(3):
        part = w.astype(ml_dtypes.bfloat16)
        parts.append(part)
        w = w - part.astype(np.float32)
    return np.stack(parts)


def tables():
    fwd, inv = dft(-1), dft(1)
    i16, i32 = np.arange(Y), np.arange(Z)
    w1, w2, w3, w3i, w4, w5 = [], [], [], [], [], []
    for a in range(NPY):
        to = [Y * ((a + r) % Q) + i16 for r in range(Q)]
        frm = [Y * ((a - r) % Q) + i16 for r in range(Q)]
        out = np.stack([fwd[:, k] for k in to]).reshape(Q, 2, Q, Q, 2, N)
        w1.append(out.transpose(Q, 5, 0, 2, 3, 1).reshape(L, L))
        inn = np.stack([inv[:, :, :, k] for k in frm]).reshape(Q, 2, N, 2, Q, Q)
        w5.append(inn.transpose(Q, 0, 5, 3, 1, 2).reshape(L, L))
        for b in range(NPZ):
            half = [Z * (b ^ q) + i32 for q in range(2)]
            m = np.stack([fwd[:, k] for k in half])
            m = np.stack([m[..., y] for y in frm])
            w2.append(m.transpose(1, 2, 3, 0, Q, 5).reshape(L, L))
            m = np.stack([inv[:, y] for y in to])
            m = np.stack([m[..., k] for k in half])
            w4.append(m.transpose(1, 2, 3, 0, Q, 5).reshape(L, L))
    for b in range(NPZ):
        half = [Z * (b ^ q) + i32 for q in range(2)]
        m = np.stack([fwd[..., z] for z in half])
        w3.append(m.transpose(0, 3, Q, 1, 2).reshape(L, L))
        m = np.stack([inv[:, z] for z in half])
        w3i.append(m.transpose(3, Q, 0, 1, 2).reshape(L, L))
    return [np.stack([split_np(w) for w in ws]) for ws in (w1, w2, w3, w3i, w4, w5)]


def split3(x):
    hi = x.astype(BF16)
    rest = x - hi.astype(F32)
    mid = rest.astype(BF16)
    return hi, mid, (rest - mid.astype(F32)).astype(BF16)


def dot(a, b):
    return jnp.dot(a, b, preferred_element_type=F32)


def left(w, x):
    hi, mid, lo = split3(x)
    wide = dot(w[0][...], jnp.concatenate([hi, mid], 0))
    return wide[:L] + (wide[L:] + dot(w[1][...], jnp.concatenate([hi, lo], 0)))


def right(x, w):
    hi, mid, lo = split3(x)
    wide = dot(jnp.concatenate([hi, mid], 1), w[0][...])
    return wide[:, :L] + (wide[:, L:] + dot(jnp.concatenate([hi, lo], 1), w[1][...]))


def left_table(w1, w2, w3):
    pairs = [jnp.concatenate([a, b], 1) for a, b in ((w1, w1), (w2, w2), (w3, w1))]
    return jnp.concatenate(pairs[:2], 0), pairs[2]


def right_table(w1, w2, w3):
    return jnp.concatenate([jnp.concatenate([w1, w2], 1)] * 2, 0), jnp.concatenate([w3, w1], 1)


def from_wide(w):
    return jnp.concatenate([w[:, :L], w[:, L:]], 0)


def swap_lanes(tiles):
    lane = lax.broadcasted_iota(jnp.int32, tiles[0].shape, 1)
    odd, high = (lane // Z) % 2 == 1, lane >= H
    t = list(tiles)
    for lo in (0, 2):
        a, b = t[lo], t[lo + 1]
        t[lo] = jnp.where(odd, pltpu.roll(b, Z, 1), a)
        t[lo + 1] = jnp.where(odd, b, pltpu.roll(a, 96, 1))
    for lo in (0, 1):
        a, b = t[lo], t[lo + 2]
        t[lo] = jnp.where(high, pltpu.roll(b, H, 1), a)
        t[lo + 2] = jnp.where(high, b, pltpu.roll(a, H, 1))
    return t


def kernel(rho_re, rho_im, g_re, g_im, t1, t2, t3, t3i, t4, t5, d_recv, hat_re, hat_im,
           rin, gin, wraw, wbig, wsmall, ga, gb, a_send, a_recv, b_send, b_recv, c_send, c_recv, d_send,
           in_sem, first_sem, g_sem, w_sem, as_sem, ar_sem, half_sem, bh_sem, bs_sem, br_sem, cs_sem, cr_sem, part_sem,
           ds_sem, dr_sem):
    me, mz = lax.axis_index("py"), lax.axis_index("pz")
    zero = lax.axis_index("dp")

    def py_peer(r):
        return (zero, mz, lax.rem(me + r, NPY))

    pz_peer = (zero, 1 - mz, me)

    def load_in(g):
        slot = lax.rem(g, 2)
        return [pltpu.make_async_copy(src.at[pl.ds(g * FG, FG)], rin.at[slot, i], in_sem.at[slot])
                for i, src in enumerate((rho_re, rho_im))]

    def inputs_of(g):
        ref = rin.at[lax.rem(g, 2)]
        pltpu.make_async_copy(ref, ref, in_sem.at[lax.rem(g, 2)]).wait()

    def load_first(q):
        ys = pl.ds(q * Q, Q)
        return [pltpu.make_async_copy(src.at[pl.ds(0, FG), ys], rin.at[0, i, :, ys], first_sem.at[q])
                for i, src in enumerate((rho_re, rho_im))]

    def first_loaded(q):
        ref = rin.at[0, :, :, pl.ds(q * Q, Q)]
        return pltpu.make_async_copy(ref, ref, first_sem.at[q])

    barrier = pltpu.get_barrier_semaphore()
    for peer in [py_peer(r) for r in (1, 2, 3)] + [pz_peer]:
        pl.semaphore_signal(barrier, inc=1, device_id=peer, device_id_type=MESH)
    both = me * NPZ + mz
    tabs = [pltpu.make_async_copy(t.at[i], wraw.at[k], w_sem.at[min(k, 1)])
            for k, (t, i) in enumerate(((t1, me), (t2, both), (t3, mz), (t3i, mz), (t4, both), (t5, me)))]
    greens = [pltpu.make_async_copy(src, gin.at[i], g_sem) for i, src in enumerate((g_re, g_im))]
    firsts = [cp for q in range(Q) for cp in load_first(q)]
    for cp in tabs[:1] + firsts + tabs[1:] + greens + load_in(1):
        cp.start()

    def table(k):
        wide, narrow = (left_table if k in (1, Q) else right_table)(*(wraw[k, i] for i in range(3)))
        wbig[k] = wide
        wsmall[k] = narrow

    def lmat(k):
        return wbig.at[k], wsmall.at[k]

    def rmat(k):
        return wbig[k], from_wide(wsmall[k])

    def stage1(g, y0, ny):
        slot, ring = lax.rem(g, 2), lax.rem(g, RA)
        w = rmat(0)
        for i in range(ny):
            y = y0 + i
            x = jnp.concatenate([rin[slot, 0, :, y].reshape(L, N), rin[slot, 1, :, y].reshape(L, N)], 1)
            out = right(x, w).T
            rows = pl.ds(pl.multiple_of(y * S, S), S)
            for c in range(Q):
                for r in range(Q):
                    tile = out[(r * Q + c) * S:(r * Q + c + 1) * S]
                    if r == 0:
                        a_recv[lax.rem(g * Q + c, AR), 0, rows, :] = tile
                    else:
                        a_send[ring, c, r - 1, rows, :] = tile

    def a_copy(u, r):
        g, c = u // Q, lax.rem(u, Q)
        ring = lax.rem(g, RA)
        return pltpu.make_async_remote_copy(
            src_ref=a_send.at[ring, c, r - 1], dst_ref=a_recv.at[lax.rem(u, AR), r], send_sem=as_sem.at[ring],
            recv_sem=ar_sem.at[lax.rem(u, AR)], device_id=py_peer(r), device_id_type=MESH)

    def a_half(u, r, h, y0, ny):
        part = (pl.ds(y0, ny), pl.ds(Q * h, Q))
        src, dst = (ref.reshape(Y, S, L).at[part] for ref in (a_send.at[0, u, r - 1], a_recv.at[u, r]))
        return pltpu.make_async_remote_copy(
            src_ref=src, dst_ref=dst, send_sem=as_sem.at[0], recv_sem=half_sem.at[u, h],
            device_id=py_peer(r), device_id_type=MESH)

    def half_arrived(u, h):
        ref = a_recv.at[u, pl.ds(1, 3), pl.ds(H * h, H)]
        return pltpu.make_async_copy(ref, ref, half_sem.at[u, h])

    def c_part(u, kk):
        ring = lax.rem(u, RING)
        return pltpu.make_async_remote_copy(
            src_ref=c_send.at[ring, kk], dst_ref=c_recv.at[lax.rem(u, RECV), 1, kk], send_sem=cs_sem.at[ring],
            recv_sem=part_sem.at[u - (NU - LATE), kk], device_id=pz_peer, device_id_type=MESH)

    def d_part(u, r, kk):
        part = (slice(None), pl.ds(2 * kk, 2))
        src, dst = (ref.reshape(Y, S, L).at[part] for ref in (d_send.at[u % RING, r - 1], d_recv.at[u, r]))
        return pltpu.make_async_remote_copy(
            src_ref=src, dst_ref=dst, send_sem=ds_sem.at[u % RING], recv_sem=dr_sem.at[(NG - 1) % RG],
            device_id=py_peer(r), device_id_type=MESH)

    def a_sent(g):
        ring = lax.rem(g, RA)
        return pltpu.make_async_copy(a_send.at[ring], a_send.at[ring], as_sem.at[ring])

    def a_arrived(u):
        ref = a_recv.at[lax.rem(u, AR), pl.ds(1, 3)]
        return pltpu.make_async_copy(ref, ref, ar_sem.at[lax.rem(u, AR)])

    def d_sent(u):
        ring = lax.rem(u, RING)
        return pltpu.make_async_copy(d_send.at[ring], d_send.at[ring], ds_sem.at[ring])

    def d_arrived(g):
        ref = d_recv.at[pl.ds(g * Q, Q), pl.ds(1, 3)]
        return pltpu.make_async_copy(ref, ref, dr_sem.at[lax.rem(g, RG)])

    def b_copy(u):
        ring = lax.rem(u, RING)
        return pltpu.make_async_remote_copy(
            src_ref=b_send.at[ring], dst_ref=b_recv.at[lax.rem(u, RECV), 1], send_sem=bs_sem.at[ring], recv_sem=br_sem.at[lax.rem(u, RECV)],
            device_id=pz_peer, device_id_type=MESH)

    def b_half(u, h):
        kk = pl.ds(2 * h, 2)
        return pltpu.make_async_remote_copy(
            src_ref=b_send.at[u, kk], dst_ref=b_recv.at[lax.rem(u, RECV), 1, kk], send_sem=bs_sem.at[u],
            recv_sem=bh_sem.at[h] if u == 0 else br_sem.at[u], device_id=pz_peer, device_id_type=MESH)

    def bh_arrived(h):
        ref = b_recv.at[0, 1, pl.ds(2 * h, 2)]
        return pltpu.make_async_copy(ref, ref, bh_sem.at[h])

    def c_half(h):
        kk = pl.ds(2 * h, 2)
        return pltpu.make_async_remote_copy(
            src_ref=c_send.at[0, kk], dst_ref=c_recv.at[0, 1, kk], send_sem=cs_sem.at[0], recv_sem=cr_sem.at[0],
            device_id=pz_peer, device_id_type=MESH)

    def c_copy(u):
        ring = lax.rem(u, RING)
        return pltpu.make_async_remote_copy(
            src_ref=c_send.at[ring], dst_ref=c_recv.at[lax.rem(u, RECV), 1], send_sem=cs_sem.at[ring], recv_sem=cr_sem.at[lax.rem(u, RECV)],
            device_id=pz_peer, device_id_type=MESH)

    def d_copy(u, r):
        ring = lax.rem(u, RING)
        return pltpu.make_async_remote_copy(
            src_ref=d_send.at[ring, r - 1], dst_ref=d_recv.at[u, r], send_sem=ds_sem.at[ring],
            recv_sem=dr_sem.at[lax.rem(u // Q, RG)], device_id=py_peer(r), device_id_type=MESH)

    def send_a(g):
        for c in range(Q):
            for r in (2, 1, 3):
                a_copy(g * Q + c, r).start()

    def y_lines(u, kp):
        ring = lax.rem(u, RING)
        cols = [jnp.concatenate([a_recv[lax.rem(u, AR), r, pl.ds(kk * 2 + ri, Y, stride=S), :]
                                 for r in range(Q) for ri in range(2)], 0) for kk in (2 * kp, 2 * kp + 1)]
        out = left(lmat(1), jnp.concatenate(cols, 1))
        for i in range(2):
            kk = 2 * kp + i
            b_recv[lax.rem(u, RECV), 0, kk] = out[:H, i * L:(i + 1) * L]
            b_send[ring, kk] = out[H:, i * L:(i + 1) * L]

    def stage2(u):
        a_arrived(u).wait()

        @pl.when(u >= RING)
        def _():
            b_copy(u - RING).wait_send()

        for kp in range(2):
            y_lines(u, kp)
        b_copy(u).start()

    def z_lines(u, kp):
        ring, c, f0 = lax.rem(u, RING), lax.rem(u, Q), u // Q * FG
        wf, wi = rmat(2), rmat(3)
        rows = []
        for kk in (2 * kp, 2 * kp + 1):
            rows += swap_lanes([b_recv[lax.rem(u, RECV), q, kk, ri * Z:(ri + 1) * Z, :] for q in range(2) for ri in range(2)])
        spec = right(jnp.concatenate(rows, 0), wf)
        hats = []
        for i in range(2):
            kk = 2 * kp + i
            gr = pl.ds(pl.multiple_of((c * Q + kk) * Z, Z), Z)
            gan, gbn = ga[gr, :], gb[gr, :]
            for f in range(FG):
                s = spec[(i * FG + f) * Z:(i * FG + f + 1) * Z]
                h = s * gan + pltpu.roll(s, H, 1) * gbn
                hat_re[f0 + f, c * Q + kk] = h[:, :N]
                hat_im[f0 + f, c * Q + kk] = h[:, N:]
                hats.append(h)
        back = right(jnp.concatenate(hats, 0), wi)
        for i in range(2):
            kk = 2 * kp + i
            t = swap_lanes([back[(i * FG + f) * Z:(i * FG + f + 1) * Z] for f in range(FG)])
            for ri in range(2):
                c_recv[lax.rem(u, RECV), 0, kk, ri * Z:(ri + 1) * Z, :] = t[ri]
                c_send[ring, kk, ri * Z:(ri + 1) * Z, :] = t[2 + ri]

    def stage3(u):
        b_copy(u).wait_recv()

        @pl.when(u >= RING)
        def _():
            c_copy(u - RING).wait_send()

        for kp in range(2):
            z_lines(u, kp)

        @pl.when(u < NU - LATE)
        def _():
            c_copy(u).start()

        @pl.when(u >= NU - LATE)
        def _():
            for kk in range(Q):
                c_part(u, kk).start()

    def y_lines_back(u, kks):
        ring = lax.rem(u, RING)
        cols = [jnp.concatenate([c_recv[lax.rem(u, RECV), q, kk] for q in range(2)], 0) for kk in kks]
        out = left(lmat(Q), jnp.concatenate(cols, 1))
        for i, kk in enumerate(kks):
            for r in range(Q):
                for ro in range(2):
                    rows = pl.ds(kk * 2 + ro, Y, stride=S)
                    tile = out[(r * 2 + ro) * Y:(r * 2 + ro + 1) * Y, i * L:(i + 1) * L]
                    if r == 0:
                        d_recv[u, 0, rows, :] = tile
                    else:
                        d_send[ring, r - 1, rows, :] = tile

    def stage4(u):
        c_copy(u).wait_recv()

        @pl.when(u >= RING)
        def _():
            d_sent(u - RING).wait()

        for kp in range(2):
            y_lines_back(u, (2 * kp, 2 * kp + 1))
        for r in (2, 1, 3):
            d_copy(u, r).start()

    def stage5(g, y0, ny):
        w = rmat(5)
        for i in range(ny):
            y = y0 + i
            rows = pl.ds(pl.multiple_of(y * S, S), S)
            x = jnp.concatenate([d_recv[g * Q + c, r, rows, :] for c in range(Q) for r in range(Q)], 0)
            out = right(x.T, w)
            for f in range(FG):
                for r in range(Q):
                    d_recv[g * Q + f, r, rows, :] = out[(f * Q + r) * S:(f * Q + r + 1) * S]

    tabs[0].wait()
    table(0)
    for q in range(Q):
        first_loaded(q).wait()
        stage1(0, q * Q, Q)
        if q == 0:
            pl.semaphore_wait(barrier, Q)
        for r in (2, 1, 3):
            a_half(0, r, 0, q * Q, Q).start()
    for u, h in [(0, 1)] + [(u, h) for u in range(1, EARLY) for h in range(2)]:
        for r in (2, 1, 3):
            a_half(u, r, h, 0, Y).start()
    for u in range(EARLY, Q):
        for r in (2, 1, 3):
            a_copy(u, r).start()
    for cp in load_in(2):
        cp.start()
    pltpu.make_async_copy(wraw.at[pl.ds(1, 5)], wraw.at[pl.ds(1, 5)], w_sem.at[1]).wait()
    for k in range(1, 6):
        table(k)
    pltpu.make_async_copy(gin, gin, g_sem).wait()
    gr, gi = gin[0].reshape(512, N), gin[1].reshape(512, N)
    ga[...] = jnp.concatenate([gr, gr], 1)
    gb[...] = jnp.concatenate([-gi, gi], 1)
    inputs_of(1)

    @pl.loop(0, Q)
    def _(q):
        stage1(1, q * Q, Q)

    send_a(1)
    for cp in load_in(3):
        cp.start()
    for u in range(EARLY):
        for h in range(2):
            half_arrived(u, h).wait()
            y_lines(u, h)
            b_half(u, h).start()
    for h in range(2):
        bh_arrived(h).wait()
        z_lines(0, h)
        c_half(h).start()


    inputs_of(2)
    for q in range(EARLY):
        stage1(2, q * Q, Q)

    def step(t, carry):
        c = lax.rem(t, Q)
        g1 = t // Q + 2

        @pl.when(t < NU)
        def _():
            stage2(t)

        u3 = t - LAG3

        @pl.when(u3 >= 1)
        def _():
            stage3(u3)

        u4 = t - LAG4

        @pl.when(u4 >= 0)
        def _():
            stage4(u4)

        @pl.when(g1 < NG)
        def _():
            @pl.when(c == 0)
            def _():
                inputs_of(g1)

                @pl.when(g1 >= RA)
                def _():
                    a_sent(g1 - RA).wait()

            stage1(g1, c * Q, Q)

            @pl.when(c == 3)
            def _():
                send_a(g1)

                @pl.when(g1 + 2 < NG)
                def _():
                    for cp in load_in(g1 + 2):
                        cp.start()

        u5 = t - LAG5

        @pl.when(u5 >= 0)
        def _():
            @pl.when(lax.rem(u5, Q) == 0)
            def _():
                d_arrived(u5 // Q).wait()

            stage5(u5 // Q, lax.rem(u5, Q) * Q, Q)

        return carry

    steps = NU - LATE + LAG4
    lax.fori_loop(EARLY, steps, step, 0)
    rest = [u5 for u5 in range(steps - LAG5, NU - Q)]
    u3 = [u for u in range(steps - LAG3, NU)]
    for u in range(NU - LATE, NU):
        if u3:
            stage3(u3.pop(0))
        d_sent(u - RING).wait()
        for kk in range(Q):
            c_part(u, kk).wait_recv()
            y_lines_back(u, (kk,))
            for r in (2, 1, 3):
                d_part(u, r, kk).start()
        for u5 in rest[:2]:
            if u5 % Q == 0:
                d_arrived(u5 // Q).wait()
            stage5(u5 // Q, u5 % Q * Q, Q)
        rest = rest[2:]
    d_arrived(NG - 1).wait()

    for g in range(NG - RA, NG):
        a_sent(g).wait()
    for u in range(NU - RING, NU):
        b_copy(u).wait_send()
        c_copy(u).wait_send()
        d_sent(u).wait()


def unpack(phi, re, im, t5, phi_re, phi_im, hat_re, hat_im, wraw, st, st_last, w_sem, hat_sem, sem, last_sem):
    tab = pltpu.make_async_copy(t5.at[lax.axis_index("py")], wraw, w_sem)
    tab.start()
    hats, phis = ((re, hat_re), (im, hat_im)), (phi_re, phi_im)
    for i in range(FIELDS // HB):
        part = pl.ds(i * HB, HB)
        for k, (src, dst) in enumerate(hats):
            pltpu.make_async_copy(src.at[part], dst.at[part], hat_sem.at[k]).start()

    def last_copy(k):
        return pltpu.make_async_copy(st_last.at[k], phis[k].at[pl.ds(FIELDS - FG, FG)], last_sem.at[k])

    tab.wait()
    wide, narrow = right_table(*(wraw[i] for i in range(3)))
    w = wide, from_wide(narrow)

    @pl.loop(0, Q)
    def _(q):
        for i in range(Q):
            y = q * Q + i
            rows = pl.ds(pl.multiple_of(y * S, S), S)
            x = jnp.concatenate([phi[NU - Q + c, r, rows, :] for c in range(Q) for r in range(Q)], 0)
            out = right(x.T, w)
            for k, half in enumerate((out[:, :N], out[:, N:])):
                st_last[k, :, y] = half.reshape(FG, Z, N)

    for k in range(2):
        last_copy(k).start()

    def copy(i, k):
        slot = lax.rem(i, SLOTS)
        return pltpu.make_async_copy(st.at[slot, k], phis[k].at[pl.ds(i * FB, FB)], sem.at[slot, k])

    def phi_job(i, carry):
        slot = lax.rem(i, SLOTS)

        @pl.when(i >= SLOTS)
        def _():
            for k in range(2):
                copy(i - SLOTS, k).wait()

        for f in range(FB):
            for r in range(Q):
                p = phi[i * FB + f, r]
                for k, half in enumerate((p[:, :N], p[:, N:])):
                    st[slot, k, f, :, r * S:(r + 1) * S] = half.reshape(Y, S, N)
        for k in range(2):
            copy(i, k).start()
        return carry

    jobs = (FIELDS - FG) // FB
    lax.fori_loop(0, jobs, phi_job, 0)
    for k, (src, dst) in enumerate(hats):
        pltpu.make_async_copy(src, dst, hat_sem.at[k]).wait()
        last_copy(k).wait()
    for i in range(jobs - SLOTS, jobs):
        for k in range(2):
            copy(i, k).wait()


def in_hbm(x):
    return pltpu.with_memory_space_constraint(x, pltpu.HBM)


def solution(mesh):
    consts = tables()

    def local_solve(rho_re, rho_im, g_re, g_im):
        dma, vmem, hbm = pltpu.SemaphoreType.DMA, pltpu.VMEM, pl.BlockSpec(memory_space=pl.ANY)
        tabs = [jnp.asarray(c) for c in consts]
        field = jax.ShapeDtypeStruct((FIELDS, Y, Z, N), F32)
        packed = pl.pallas_call(
            kernel,
            out_shape=[pltpu.VMEM((NU, Q, L, L), F32)] + [pltpu.VMEM(field.shape, F32)] * 2,
            in_specs=[hbm] * 10,
            out_specs=[pl.BlockSpec(memory_space=pltpu.VMEM)] * 3,
            scratch_shapes=[
                vmem((2, 2, FG, Y, Z, N), F32),
                vmem((2, Y, Z, N), F32),
                vmem((6, 3, L, L), BF16),
                vmem((6, 256, 256), BF16),
                vmem((6, L, 256), BF16),
                vmem((512, L), F32), vmem((512, L), F32),
                vmem((RA, Q, 3, L, L), F32),
                vmem((AR, Q, L, L), F32),
                vmem((RING, Q, H, L), F32),
                vmem((RECV, 2, Q, H, L), F32),
                vmem((RING, Q, H, L), F32),
                vmem((RECV, 2, Q, H, L), F32),
                vmem((RING, 3, L, L), F32),
                dma((2,)), dma((Q,)), dma, dma((2,)), dma((RA,)), dma((AR,)), dma((EARLY, 2)), dma((2,)),
                dma((RING,)), dma((RECV,)), dma((RING,)), dma((RECV,)), dma((LATE, Q)), dma((RING,)), dma((RG,)),
            ],
            compiler_params=pltpu.CompilerParams(collective_id=0, has_side_effects=True,
                                                 vmem_limit_bytes=24 << 20),
            name="spectral",
        )(*(in_hbm(x) for x in (jnp.transpose(rho_re, (0, 2, 3, 1)), jnp.transpose(rho_im, (0, 2, 3, 1)), g_re, g_im, *tabs)))
        packed = [pltpu.with_memory_space_constraint(x, pltpu.VMEM) for x in packed]
        phi_re, phi_im, hat_re, hat_im = pl.pallas_call(
            unpack,
            out_shape=[field] * Q,
            in_specs=[pl.BlockSpec(memory_space=pltpu.VMEM)] * 3 + [hbm],
            out_specs=[hbm] * Q,
            scratch_shapes=[vmem((3, L, L), BF16), vmem((SLOTS, 2, FB, Y, Z, N), F32),
                            vmem((2, FG, Y, Z, N), F32), dma, dma((2,)), dma((SLOTS, 2)), dma((2,))],
            compiler_params=pltpu.CompilerParams(vmem_limit_bytes=20 << 20),
            name="unpack",
        )(*packed, in_hbm(tabs[5]))
        return jnp.transpose(phi_re, (0, 3, 1, 2)), jnp.transpose(phi_im, (0, 3, 1, 2)), hat_re, hat_im

    space_layout = P("dp", None, "py", "pz")
    wave_layout = P("dp", "py", "pz", None)
    green_layout = P("py", "pz", None)
    return jax.shard_map(local_solve, mesh=mesh,
                         in_specs=(space_layout, space_layout, green_layout, green_layout),
                         out_specs=(space_layout, space_layout, wave_layout, wave_layout),
                         check_vma=False)
```

time: 207 us -> 206 us (level)
  no operation moved by 1% of the time
where the time goes in v5:
time: 206 us
  Pallas kernels  205 us (100%)
    pallas_call x1, Pallas kernels, local_solve(): pl.pallas_call(kernel, out_shape=[pltpu.VMEM((NU, Q, L, L), F32)] + [pltp...  194 us
    pallas_call x1, Pallas kernels, local_solve(): pl.pallas_call(unpack, out_shape=[field] * Q, in_specs=[pl.BlockSpec(memo...  11 us

profile of v5, /device:TPU:0, one launch (start us, length us, event | category | flops | bytes accessed | tf_op | source)
XLA Modules:
  0.0 205.7 jit_solution(5271331551861430671)
XLA Ops:
  0.6 194.1 %spectral.1 = (f32[32,4,128,128]{3,2,1,0:T(8,128)S(1)}, f32[32,16,32,64]{3,2,1,0:T(8,128)S(1)}, f32[32,16,32,64]{3,2,1,0:T(8,128)S(1)}) custom-call(f32[32,16,32,64]{3,2,1,0:T(8,128)} %bitcast.4, f32[32,16,32,64]{3,2,1,0:T(8,128)} %bitcast.5, f32[16,32,64]{2,1,0:T(8,128)} %g_re.1, f32[16,32,64]{2,1,0:T(8,128)} %g_im.1, ...), custom_call_target="tpu_custom_call" | custom-call | tf_op jit(solution)/shard_map/spectral/pallas_call | solution.py:586
  194.8 11.0 %unpack.1 = (f32[32,16,32,64]{3,2,1,0:T(8,128)}, f32[32,16,32,64]{3,2,1,0:T(8,128)}, f32[32,16,32,64]{3,2,1,0:T(8,128)}, f32[32,16,32,64]{3,2,1,0:T(8,128)}) custom-call(f32[32,4,128,128]{3,2,1,0:T(8,128)S(1)} %get-tuple-element.11.phi, f32[32,16,32,64]{3,2,1,0:T(8,128)S(1)} %get-tuple-element.12.re, f32[32,16,32,64]{3,2,1,0:T(8,128)S(1)} %get-tuple-element.13.im, ...), custom_call_target="tpu_custom_call" | custom-call | tf_op jit(solution)/shard_map/unpack/pallas_call | solution.py:613

commit v6 on v5

--- a/solution.py
+++ b/solution.py
@@ -25,7 +25,10 @@
 RG = 4
 RA = 3
 AR = 16
+BLOCKS = 2
+NY = 16 // BLOCKS
 EARLY = 2
+PIECES = [(u, k) for u in range(EARLY) for k in range(4)]
 LATE = 3
 FB, SLOTS = 4, 4
 HB = 8
@@ -128,7 +131,7 @@
 
 def kernel(rho_re, rho_im, g_re, g_im, t1, t2, t3, t3i, t4, t5, d_recv, hat_re, hat_im,
            rin, gin, wraw, wbig, wsmall, ga, gb, a_send, a_recv, b_send, b_recv, c_send, c_recv, d_send,
-           in_sem, first_sem, g_sem, w_sem, as_sem, ar_sem, half_sem, bh_sem, bs_sem, br_sem, cs_sem, cr_sem, part_sem,
+           in_sem, first_sem, g_sem, w_sem, as_sem, ar_sem, piece_sem, bh_sem, bs_sem, br_sem, cs_sem, cr_sem, part_sem,
            ds_sem, dr_sem):
     me, mz = lax.axis_index("py"), lax.axis_index("pz")
     zero = lax.axis_index("dp")
@@ -148,12 +151,12 @@
         pltpu.make_async_copy(ref, ref, in_sem.at[lax.rem(g, 2)]).wait()
 
     def load_first(q):
-        ys = pl.ds(q * Q, Q)
+        ys = pl.ds(q * NY, NY)
         return [pltpu.make_async_copy(src.at[pl.ds(0, FG), ys], rin.at[0, i, :, ys], first_sem.at[q])
                 for i, src in enumerate((rho_re, rho_im))]
 
     def first_loaded(q):
-        ref = rin.at[0, :, :, pl.ds(q * Q, Q)]
+        ref = rin.at[0, :, :, pl.ds(q * NY, NY)]
         return pltpu.make_async_copy(ref, ref, first_sem.at[q])
 
     barrier = pltpu.get_barrier_semaphore()
@@ -163,7 +166,7 @@
     tabs = [pltpu.make_async_copy(t.at[i], wraw.at[k], w_sem.at[min(k, 1)])
             for k, (t, i) in enumerate(((t1, me), (t2, both), (t3, mz), (t3i, mz), (t4, both), (t5, me)))]
     greens = [pltpu.make_async_copy(src, gin.at[i], g_sem) for i, src in enumerate((g_re, g_im))]
-    firsts = [cp for q in range(Q) for cp in load_first(q)]
+    firsts = [cp for q in range(BLOCKS) for cp in load_first(q)]
     for cp in tabs[:1] + firsts + tabs[1:] + greens + load_in(1):
         cp.start()
 
@@ -201,16 +204,16 @@
             src_ref=a_send.at[ring, c, r - 1], dst_ref=a_recv.at[lax.rem(u, AR), r], send_sem=as_sem.at[ring],
             recv_sem=ar_sem.at[lax.rem(u, AR)], device_id=py_peer(r), device_id_type=MESH)
 
-    def a_half(u, r, h, y0, ny):
-        part = (pl.ds(y0, ny), pl.ds(Q * h, Q))
+    def a_piece(u, k, r, y0, ny):
+        part = (pl.ds(y0, ny), pl.ds(2 * k, 2))
         src, dst = (ref.reshape(Y, S, L).at[part] for ref in (a_send.at[0, u, r - 1], a_recv.at[u, r]))
         return pltpu.make_async_remote_copy(
-            src_ref=src, dst_ref=dst, send_sem=as_sem.at[0], recv_sem=half_sem.at[u, h],
+            src_ref=src, dst_ref=dst, send_sem=as_sem.at[0], recv_sem=piece_sem.at[u, k],
             device_id=py_peer(r), device_id_type=MESH)
 
-    def half_arrived(u, h):
-        ref = a_recv.at[u, pl.ds(1, 3), pl.ds(H * h, H)]
-        return pltpu.make_async_copy(ref, ref, half_sem.at[u, h])
+    def piece_arrived(u, k):
+        ref = a_recv.at[u, pl.ds(1, 3), pl.ds(Z * k, Z)]
+        return pltpu.make_async_copy(ref, ref, piece_sem.at[u, k])
 
     def c_part(u, kk):
         ring = lax.rem(u, RING)
@@ -247,11 +250,10 @@
             src_ref=b_send.at[ring], dst_ref=b_recv.at[lax.rem(u, RECV), 1], send_sem=bs_sem.at[ring], recv_sem=br_sem.at[lax.rem(u, RECV)],
             device_id=pz_peer, device_id_type=MESH)
 
-    def b_half(u, h):
-        kk = pl.ds(2 * h, 2)
-        return pltpu.make_async_remote_copy(
-            src_ref=b_send.at[u, kk], dst_ref=b_recv.at[lax.rem(u, RECV), 1, kk], send_sem=bs_sem.at[u],
-            recv_sem=bh_sem.at[h] if u == 0 else br_sem.at[u], device_id=pz_peer, device_id_type=MESH)
+    def b_piece(u, k):
+        return pltpu.make_async_remote_copy(
+            src_ref=b_send.at[u, k], dst_ref=b_recv.at[u, 1, k], send_sem=bs_sem.at[u],
+            recv_sem=br_sem.at[u] if u else bh_sem.at[k // 2], device_id=pz_peer, device_id_type=MESH)
 
     def bh_arrived(h):
         ref = b_recv.at[0, 1, pl.ds(2 * h, 2)]
@@ -280,14 +282,13 @@
             for r in (2, 1, 3):
                 a_copy(g * Q + c, r).start()
 
-    def y_lines(u, kp):
-        ring = lax.rem(u, RING)
-        cols = [jnp.concatenate([a_recv[lax.rem(u, AR), r, pl.ds(kk * 2 + ri, Y, stride=S), :]
-                                 for r in range(Q) for ri in range(2)], 0) for kk in (2 * kp, 2 * kp + 1)]
+    def y_lines(u, kks):
+        ring, slot, arrived = lax.rem(u, RING), lax.rem(u, RECV), lax.rem(u, AR)
+        cols = [jnp.concatenate([a_recv[arrived, r, pl.ds(kk * 2 + ri, Y, stride=S), :]
+                                 for r in range(Q) for ri in range(2)], 0) for kk in kks]
         out = left(lmat(1), jnp.concatenate(cols, 1))
-        for i in range(2):
-            kk = 2 * kp + i
-            b_recv[lax.rem(u, RECV), 0, kk] = out[:H, i * L:(i + 1) * L]
+        for i, kk in enumerate(kks):
+            b_recv[slot, 0, kk] = out[:H, i * L:(i + 1) * L]
             b_send[ring, kk] = out[H:, i * L:(i + 1) * L]
 
     def stage2(u):
@@ -298,7 +299,7 @@
             b_copy(u - RING).wait_send()
 
         for kp in range(2):
-            y_lines(u, kp)
+            y_lines(u, (2 * kp, 2 * kp + 1))
         b_copy(u).start()
 
     def z_lines(u, kp):
@@ -383,18 +384,20 @@
                 for r in range(Q):
                     d_recv[g * Q + f, r, rows, :] = out[(f * Q + r) * S:(f * Q + r + 1) * S]
 
+    odd = lax.rem(me, 2)
+    order = (2 - odd, 3 - odd, 1 + 2 * odd)
     tabs[0].wait()
     table(0)
-    for q in range(Q):
+    for q in range(BLOCKS):
         first_loaded(q).wait()
-        stage1(0, q * Q, Q)
+        stage1(0, q * NY, NY)
         if q == 0:
             pl.semaphore_wait(barrier, Q)
-        for r in (2, 1, 3):
-            a_half(0, r, 0, q * Q, Q).start()
-    for u, h in [(0, 1)] + [(u, h) for u in range(1, EARLY) for h in range(2)]:
-        for r in (2, 1, 3):
-            a_half(u, r, h, 0, Y).start()
+        for r in order:
+            a_piece(0, 0, r, q * NY, NY).start()
+    for u, k in PIECES[1:]:
+        for r in order:
+            a_piece(u, k, r, 0, Y).start()
     for u in range(EARLY, Q):
         for r in (2, 1, 3):
             a_copy(u, r).start()
@@ -416,16 +419,14 @@
     send_a(1)
     for cp in load_in(3):
         cp.start()
-    for u in range(EARLY):
-        for h in range(2):
-            half_arrived(u, h).wait()
-            y_lines(u, h)
-            b_half(u, h).start()
+    for u, k in PIECES:
+        piece_arrived(u, k).wait()
+        y_lines(u, (k,))
+        b_piece(u, k).start()
     for h in range(2):
         bh_arrived(h).wait()
         z_lines(0, h)
         c_half(h).start()
-
 
     inputs_of(2)
     for q in range(EARLY):
@@ -602,7 +603,7 @@
                 vmem((RING, Q, H, L), F32),
                 vmem((RECV, 2, Q, H, L), F32),
                 vmem((RING, 3, L, L), F32),
-                dma((2,)), dma((Q,)), dma, dma((2,)), dma((RA,)), dma((AR,)), dma((EARLY, 2)), dma((2,)),
+                dma((2,)), dma((BLOCKS,)), dma, dma((2,)), dma((RA,)), dma((AR,)), dma((EARLY, Q)), dma((2,)),
                 dma((RING,)), dma((RECV,)), dma((RING,)), dma((RECV,)), dma((LATE, Q)), dma((RING,)), dma((RG,)),
             ],
             compiler_params=pltpu.CompilerParams(collective_id=0, has_side_effects=True,

time: 206 us -> 205 us (level)
  no operation moved by 1% of the time
where the time goes in v6:
time: 205 us
  Pallas kernels  205 us (100%)
    pallas_call x1, Pallas kernels, local_solve(): pl.pallas_call(kernel, out_shape=[pltpu.VMEM((NU, Q, L, L), F32)] + [pltp...  194 us
    pallas_call x1, Pallas kernels, local_solve(): pl.pallas_call(unpack, out_shape=[field] * Q, in_specs=[pl.BlockSpec(memo...  11 us

profile of v6, /device:TPU:0, one launch (start us, length us, event | category | flops | bytes accessed | tf_op | source)
XLA Modules:
  0.0 205.2 jit_solution(4390561854497877302)
XLA Ops:
  0.6 193.6 %spectral.1 = (f32[32,4,128,128]{3,2,1,0:T(8,128)S(1)}, f32[32,16,32,64]{3,2,1,0:T(8,128)S(1)}, f32[32,16,32,64]{3,2,1,0:T(8,128)S(1)}) custom-call(f32[32,16,32,64]{3,2,1,0:T(8,128)} %bitcast.4, f32[32,16,32,64]{3,2,1,0:T(8,128)} %bitcast.5, f32[16,32,64]{2,1,0:T(8,128)} %g_re.1, f32[16,32,64]{2,1,0:T(8,128)} %g_im.1, ...), custom_call_target="tpu_custom_call" | custom-call | tf_op jit(solution)/shard_map/spectral/pallas_call | solution.py:587
  194.3 11.0 %unpack.1 = (f32[32,16,32,64]{3,2,1,0:T(8,128)}, f32[32,16,32,64]{3,2,1,0:T(8,128)}, f32[32,16,32,64]{3,2,1,0:T(8,128)}, f32[32,16,32,64]{3,2,1,0:T(8,128)}) custom-call(f32[32,4,128,128]{3,2,1,0:T(8,128)S(1)} %get-tuple-element.11.phi, f32[32,16,32,64]{3,2,1,0:T(8,128)S(1)} %get-tuple-element.12.re, f32[32,16,32,64]{3,2,1,0:T(8,128)S(1)} %get-tuple-element.13.im, ...), custom_call_target="tpu_custom_call" | custom-call | tf_op jit(solution)/shard_map/unpack/pallas_call | solution.py:614

commit v7 on v6

--- a/solution.py
+++ b/solution.py
@@ -131,7 +131,7 @@
 
 def kernel(rho_re, rho_im, g_re, g_im, t1, t2, t3, t3i, t4, t5, d_recv, hat_re, hat_im,
            rin, gin, wraw, wbig, wsmall, ga, gb, a_send, a_recv, b_send, b_recv, c_send, c_recv, d_send,
-           in_sem, first_sem, g_sem, w_sem, as_sem, ar_sem, piece_sem, bh_sem, bs_sem, br_sem, cs_sem, cr_sem, part_sem,
+           in_sem, first_sem, g_sem, w_sem, as_sem, ar_sem, bs_sem, br_sem, cs_sem, cr_sem, part_sem,
            ds_sem, dr_sem):
     me, mz = lax.axis_index("py"), lax.axis_index("pz")
     zero = lax.axis_index("dp")
@@ -208,12 +208,12 @@
         part = (pl.ds(y0, ny), pl.ds(2 * k, 2))
         src, dst = (ref.reshape(Y, S, L).at[part] for ref in (a_send.at[0, u, r - 1], a_recv.at[u, r]))
         return pltpu.make_async_remote_copy(
-            src_ref=src, dst_ref=dst, send_sem=as_sem.at[0], recv_sem=piece_sem.at[u, k],
+            src_ref=src, dst_ref=dst, send_sem=as_sem.at[0], recv_sem=part_sem.at[u, k],
             device_id=py_peer(r), device_id_type=MESH)
 
     def piece_arrived(u, k):
         ref = a_recv.at[u, pl.ds(1, 3), pl.ds(Z * k, Z)]
-        return pltpu.make_async_copy(ref, ref, piece_sem.at[u, k])
+        return pltpu.make_async_copy(ref, ref, part_sem.at[u, k])
 
     def c_part(u, kk):
         ring = lax.rem(u, RING)
@@ -253,11 +253,11 @@
     def b_piece(u, k):
         return pltpu.make_async_remote_copy(
             src_ref=b_send.at[u, k], dst_ref=b_recv.at[u, 1, k], send_sem=bs_sem.at[u],
-            recv_sem=br_sem.at[u] if u else bh_sem.at[k // 2], device_id=pz_peer, device_id_type=MESH)
+            recv_sem=br_sem.at[u] if u else part_sem.at[EARLY, k // 2], device_id=pz_peer, device_id_type=MESH)
 
     def bh_arrived(h):
         ref = b_recv.at[0, 1, pl.ds(2 * h, 2)]
-        return pltpu.make_async_copy(ref, ref, bh_sem.at[h])
+        return pltpu.make_async_copy(ref, ref, part_sem.at[EARLY, h])
 
     def c_half(h):
         kk = pl.ds(2 * h, 2)
@@ -603,7 +603,7 @@
                 vmem((RING, Q, H, L), F32),
                 vmem((RECV, 2, Q, H, L), F32),
                 vmem((RING, 3, L, L), F32),
-                dma((2,)), dma((BLOCKS,)), dma, dma((2,)), dma((RA,)), dma((AR,)), dma((EARLY, Q)), dma((2,)),
+                dma((2,)), dma((BLOCKS,)), dma, dma((2,)), dma((RA,)), dma((AR,)),
                 dma((RING,)), dma((RECV,)), dma((RING,)), dma((RECV,)), dma((LATE, Q)), dma((RING,)), dma((RG,)),
             ],
             compiler_params=pltpu.CompilerParams(collective_id=0, has_side_effects=True,

time: 205 us -> 205 us (level)
  no operation moved by 1% of the time
where the time goes in v7:
time: 205 us
  Pallas kernels  205 us (100%)
    pallas_call x1, Pallas kernels, local_solve(): pl.pallas_call(kernel, out_shape=[pltpu.VMEM((NU, Q, L, L), F32)] + [pltp...  194 us
    pallas_call x1, Pallas kernels, local_solve(): pl.pallas_call(unpack, out_shape=[field] * Q, in_specs=[pl.BlockSpec(memo...  11 us

profile of v7, /device:TPU:0, one launch (start us, length us, event | category | flops | bytes accessed | tf_op | source)
XLA Modules:
  0.0 205.2 jit_solution(6917774016366741689)
XLA Ops:
  0.6 193.5 %spectral.1 = (f32[32,4,128,128]{3,2,1,0:T(8,128)S(1)}, f32[32,16,32,64]{3,2,1,0:T(8,128)S(1)}, f32[32,16,32,64]{3,2,1,0:T(8,128)S(1)}) custom-call(f32[32,16,32,64]{3,2,1,0:T(8,128)} %bitcast.4, f32[32,16,32,64]{3,2,1,0:T(8,128)} %bitcast.5, f32[16,32,64]{2,1,0:T(8,128)} %g_re.1, f32[16,32,64]{2,1,0:T(8,128)} %g_im.1, ...), custom_call_target="tpu_custom_call" | custom-call | tf_op jit(solution)/shard_map/spectral/pallas_call | solution.py:587
  194.2 11.0 %unpack.1 = (f32[32,16,32,64]{3,2,1,0:T(8,128)}, f32[32,16,32,64]{3,2,1,0:T(8,128)}, f32[32,16,32,64]{3,2,1,0:T(8,128)}, f32[32,16,32,64]{3,2,1,0:T(8,128)}) custom-call(f32[32,4,128,128]{3,2,1,0:T(8,128)S(1)} %get-tuple-element.11.phi, f32[32,16,32,64]{3,2,1,0:T(8,128)S(1)} %get-tuple-element.12.re, f32[32,16,32,64]{3,2,1,0:T(8,128)S(1)} %get-tuple-element.13.im, ...), custom_call_target="tpu_custom_call" | custom-call | tf_op jit(solution)/shard_map/unpack/pallas_call | solution.py:614

commit v8 on v7

--- a/solution.py
+++ b/solution.py
@@ -523,7 +523,7 @@
             pltpu.make_async_copy(src.at[part], dst.at[part], hat_sem.at[k]).start()
 
     def last_copy(k):
-        return pltpu.make_async_copy(st_last.at[k], phis[k].at[pl.ds(FIELDS - FG, FG)], last_sem.at[k])
+        return pltpu.make_async_copy(st_last.at[k], phis[k].at[pl.ds(FIELDS - FG, FG)], last_sem)
 
     tab.wait()
     wide, narrow = right_table(*(wraw[i] for i in range(3)))
@@ -544,15 +544,18 @@
 
     def copy(i, k):
         slot = lax.rem(i, SLOTS)
-        return pltpu.make_async_copy(st.at[slot, k], phis[k].at[pl.ds(i * FB, FB)], sem.at[slot, k])
+        return pltpu.make_async_copy(st.at[slot, k], phis[k].at[pl.ds(i * FB, FB)], sem.at[slot])
+
+    def written(i):
+        slot = lax.rem(i, SLOTS)
+        pltpu.make_async_copy(st.at[slot], st.at[slot], sem.at[slot]).wait()
 
     def phi_job(i, carry):
         slot = lax.rem(i, SLOTS)
 
         @pl.when(i >= SLOTS)
         def _():
-            for k in range(2):
-                copy(i - SLOTS, k).wait()
+            written(i - SLOTS)
 
         for f in range(FB):
             for r in range(Q):
@@ -567,10 +570,9 @@
     lax.fori_loop(0, jobs, phi_job, 0)
     for k, (src, dst) in enumerate(hats):
         pltpu.make_async_copy(src, dst, hat_sem.at[k]).wait()
-        last_copy(k).wait()
+    pltpu.make_async_copy(st_last, st_last, last_sem).wait()
     for i in range(jobs - SLOTS, jobs):
-        for k in range(2):
-            copy(i, k).wait()
+        written(i)
 
 
 def in_hbm(x):
@@ -617,7 +619,7 @@
             in_specs=[pl.BlockSpec(memory_space=pltpu.VMEM)] * 3 + [hbm],
             out_specs=[hbm] * Q,
             scratch_shapes=[vmem((3, L, L), BF16), vmem((SLOTS, 2, FB, Y, Z, N), F32),
-                            vmem((2, FG, Y, Z, N), F32), dma, dma((2,)), dma((SLOTS, 2)), dma((2,))],
+                            vmem((2, FG, Y, Z, N), F32), dma, dma((2,)), dma((SLOTS,)), dma],
             compiler_params=pltpu.CompilerParams(vmem_limit_bytes=20 << 20),
             name="unpack",
         )(*packed, in_hbm(tabs[5]))

time: 205 us -> 205 us (level)
  no operation moved by 1% of the time
where the time goes in v8:
time: 205 us
  Pallas kernels  204 us (100%)
    pallas_call x1, Pallas kernels, local_solve(): pl.pallas_call(kernel, out_shape=[pltpu.VMEM((NU, Q, L, L), F32)] + [pltp...  194 us
    pallas_call x1, Pallas kernels, local_solve(): pl.pallas_call(unpack, out_shape=[field] * Q, in_specs=[pl.BlockSpec(memo...  10.9 us

profile of v8, /device:TPU:0, one launch (start us, length us, event | category | flops | bytes accessed | tf_op | source)
XLA Modules:
  0.0 205.1 jit_solution(3522111001360365386)
XLA Ops:
  0.6 193.5 %spectral.1 = (f32[32,4,128,128]{3,2,1,0:T(8,128)S(1)}, f32[32,16,32,64]{3,2,1,0:T(8,128)S(1)}, f32[32,16,32,64]{3,2,1,0:T(8,128)S(1)}) custom-call(f32[32,16,32,64]{3,2,1,0:T(8,128)} %bitcast.4, f32[32,16,32,64]{3,2,1,0:T(8,128)} %bitcast.5, f32[16,32,64]{2,1,0:T(8,128)} %g_re.1, f32[16,32,64]{2,1,0:T(8,128)} %g_im.1, ...), custom_call_target="tpu_custom_call" | custom-call | tf_op jit(solution)/shard_map/spectral/pallas_call | solution.py:589
  194.2 10.9 %unpack.1 = (f32[32,16,32,64]{3,2,1,0:T(8,128)}, f32[32,16,32,64]{3,2,1,0:T(8,128)}, f32[32,16,32,64]{3,2,1,0:T(8,128)}, f32[32,16,32,64]{3,2,1,0:T(8,128)}) custom-call(f32[32,4,128,128]{3,2,1,0:T(8,128)S(1)} %get-tuple-element.11.phi, f32[32,16,32,64]{3,2,1,0:T(8,128)S(1)} %get-tuple-element.12.re, f32[32,16,32,64]{3,2,1,0:T(8,128)S(1)} %get-tuple-element.13.im, ...), custom_call_target="tpu_custom_call" | custom-call | tf_op jit(solution)/shard_map/unpack/pallas_call | solution.py:616

commit v9 on v8

--- a/solution.py
+++ b/solution.py
@@ -20,7 +20,7 @@
 NPY, NPZ = 4, 2
 LAG3, LAG4 = 2, 4
 LAG5 = LAG4 + 5
-RING = 4
+RING = 3
 RECV = 6
 RG = 4
 RA = 3

time: 205 us -> 205 us (level)
  no operation moved by 1% of the time
where the time goes in v9:
time: 205 us
  Pallas kernels  204 us (100%)
    pallas_call x1, Pallas kernels, local_solve(): pl.pallas_call(kernel, out_shape=[pltpu.VMEM((NU, Q, L, L), F32)] + [pltp...  194 us
    pallas_call x1, Pallas kernels, local_solve(): pl.pallas_call(unpack, out_shape=[field] * Q, in_specs=[pl.BlockSpec(memo...  10.9 us

profile of v9, /device:TPU:0, one launch (start us, length us, event | category | flops | bytes accessed | tf_op | source)
XLA Modules:
  0.0 205.1 jit_solution(1311059053605950022)
XLA Ops:
  0.6 193.5 %spectral.1 = (f32[32,4,128,128]{3,2,1,0:T(8,128)S(1)}, f32[32,16,32,64]{3,2,1,0:T(8,128)S(1)}, f32[32,16,32,64]{3,2,1,0:T(8,128)S(1)}) custom-call(f32[32,16,32,64]{3,2,1,0:T(8,128)} %bitcast.4, f32[32,16,32,64]{3,2,1,0:T(8,128)} %bitcast.5, f32[16,32,64]{2,1,0:T(8,128)} %g_re.1, f32[16,32,64]{2,1,0:T(8,128)} %g_im.1, ...), custom_call_target="tpu_custom_call" | custom-call | tf_op jit(solution)/shard_map/spectral/pallas_call | solution.py:589
  194.1 10.9 %unpack.1 = (f32[32,16,32,64]{3,2,1,0:T(8,128)}, f32[32,16,32,64]{3,2,1,0:T(8,128)}, f32[32,16,32,64]{3,2,1,0:T(8,128)}, f32[32,16,32,64]{3,2,1,0:T(8,128)}) custom-call(f32[32,4,128,128]{3,2,1,0:T(8,128)S(1)} %get-tuple-element.11.phi, f32[32,16,32,64]{3,2,1,0:T(8,128)S(1)} %get-tuple-element.12.re, f32[32,16,32,64]{3,2,1,0:T(8,128)S(1)} %get-tuple-element.13.im, ...), custom_call_target="tpu_custom_call" | custom-call | tf_op jit(solution)/shard_map/unpack/pallas_call | solution.py:616

commit v10 on v9

--- a/solution.py
+++ b/solution.py
@@ -513,7 +513,7 @@
         d_sent(u).wait()
 
 
-def unpack(phi, re, im, t5, phi_re, phi_im, hat_re, hat_im, wraw, st, st_last, w_sem, hat_sem, sem, last_sem):
+def unpack(phi, re, im, t5, phi_re, phi_im, hat_re, hat_im, wraw, st, st_last, w_sem, hat_sem, sem):
     tab = pltpu.make_async_copy(t5.at[lax.axis_index("py")], wraw, w_sem)
     tab.start()
     hats, phis = ((re, hat_re), (im, hat_im)), (phi_re, phi_im)
@@ -523,7 +523,7 @@
             pltpu.make_async_copy(src.at[part], dst.at[part], hat_sem.at[k]).start()
 
     def last_copy(k):
-        return pltpu.make_async_copy(st_last.at[k], phis[k].at[pl.ds(FIELDS - FG, FG)], last_sem)
+        return pltpu.make_async_copy(st_last.at[k], phis[k].at[pl.ds(FIELDS - FG, FG)], w_sem)
 
     tab.wait()
     wide, narrow = right_table(*(wraw[i] for i in range(3)))
@@ -570,7 +570,7 @@
     lax.fori_loop(0, jobs, phi_job, 0)
     for k, (src, dst) in enumerate(hats):
         pltpu.make_async_copy(src, dst, hat_sem.at[k]).wait()
-    pltpu.make_async_copy(st_last, st_last, last_sem).wait()
+    pltpu.make_async_copy(st_last, st_last, w_sem).wait()
     for i in range(jobs - SLOTS, jobs):
         written(i)
 
@@ -619,7 +619,7 @@
             in_specs=[pl.BlockSpec(memory_space=pltpu.VMEM)] * 3 + [hbm],
             out_specs=[hbm] * Q,
             scratch_shapes=[vmem((3, L, L), BF16), vmem((SLOTS, 2, FB, Y, Z, N), F32),
-                            vmem((2, FG, Y, Z, N), F32), dma, dma((2,)), dma((SLOTS,)), dma],
+                            vmem((2, FG, Y, Z, N), F32), dma, dma((2,)), dma((SLOTS,))],
             compiler_params=pltpu.CompilerParams(vmem_limit_bytes=20 << 20),
             name="unpack",
         )(*packed, in_hbm(tabs[5]))

time: 205 us -> 205 us (level)
  no operation moved by 1% of the time
where the time goes in v10:
time: 205 us
  Pallas kernels  204 us (100%)
    pallas_call x1, Pallas kernels, local_solve(): pl.pallas_call(kernel, out_shape=[pltpu.VMEM((NU, Q, L, L), F32)] + [pltp...  194 us
    pallas_call x1, Pallas kernels, local_solve(): pl.pallas_call(unpack, out_shape=[field] * Q, in_specs=[pl.BlockSpec(memo...  10.9 us

profile of v10, /device:TPU:0, one launch (start us, length us, event | category | flops | bytes accessed | tf_op | source)
XLA Modules:
  0.0 205.1 jit_solution(16531179830660214515)
XLA Ops:
  0.6 193.5 %spectral.1 = (f32[32,4,128,128]{3,2,1,0:T(8,128)S(1)}, f32[32,16,32,64]{3,2,1,0:T(8,128)S(1)}, f32[32,16,32,64]{3,2,1,0:T(8,128)S(1)}) custom-call(f32[32,16,32,64]{3,2,1,0:T(8,128)} %bitcast.4, f32[32,16,32,64]{3,2,1,0:T(8,128)} %bitcast.5, f32[16,32,64]{2,1,0:T(8,128)} %g_re.1, f32[16,32,64]{2,1,0:T(8,128)} %g_im.1, ...), custom_call_target="tpu_custom_call" | custom-call | tf_op jit(solution)/shard_map/spectral/pallas_call | solution.py:589
  194.1 10.9 %unpack.1 = (f32[32,16,32,64]{3,2,1,0:T(8,128)}, f32[32,16,32,64]{3,2,1,0:T(8,128)}, f32[32,16,32,64]{3,2,1,0:T(8,128)}, f32[32,16,32,64]{3,2,1,0:T(8,128)}) custom-call(f32[32,4,128,128]{3,2,1,0:T(8,128)S(1)} %get-tuple-element.11.phi, f32[32,16,32,64]{3,2,1,0:T(8,128)S(1)} %get-tuple-element.12.re, f32[32,16,32,64]{3,2,1,0:T(8,128)S(1)} %get-tuple-element.13.im, ...), custom_call_target="tpu_custom_call" | custom-call | tf_op jit(solution)/shard_map/unpack/pallas_call | solution.py:616
